TPU v7x, 16 devices: a whole 2x2x2 slice. The times are simulated.
16 devices in a mesh: dp: 4 (over z, y), ep: 4 (over x, core).
Axes of the slice: x: 2, y: 2, z: 2, core: 2. Of those that a mesh axis runs over, the one named last changes fastest.
Arguments:
- h0: bfloat16 [16, 256, 2048], P(('dp', 'ep')), parts along dimension 0
- idx: int32 [16, 256, 6], P(('dp', 'ep')), parts along dimension 0
- slot: int32 [16, 256, 6], P(('dp', 'ep')), parts along dimension 0
- ln_attn: bfloat16 [2048], replicated
- wq: bfloat16 [2048, 2048], replicated
- wk: bfloat16 [2048, 2048], replicated
- wv: bfloat16 [2048, 2048], replicated
- wo: bfloat16 [2048, 2048], replicated
- ln_ffn: bfloat16 [2048], replicated
- ws1: bfloat16 [2048, 2816], replicated
- ws3: bfloat16 [2048, 2816], replicated
- ws2: bfloat16 [2816, 2048], replicated
- ln_moe: bfloat16 [2048], replicated
- wr: bfloat16 [2048, 64], replicated
- ue1: bfloat16 [64, 2048, 1408], P('ep')
- ue3: bfloat16 [64, 2048, 1408], P('ep')
- ue2: bfloat16 [64, 1408, 2048], P('ep')
Outputs:
- output: bfloat16 [16, 256, 2048], P(('dp', 'ep')), parts along dimension 0
There are 4 independent parts. A program takes and returns all parts, laid end to end along the dimension named above; an argument that names none is the same for every part.
All inputs are finite; a program needn't handle non-finite values.
Results may differ from a plain program's by a relative error of at most 0.00929055.
Values are sent between devices in bfloat16 or wider.
A program may use at most 1.5 GiB of HBM per device.

v0:
```python
import jax
import jax.numpy as jnp
from jax import lax
from jax.sharding import PartitionSpec as P

HEAD = 128
EPS = 1e-6
CAP_FACTOR = 2


def _mm(form, a, b):
    return jnp.einsum(form, a, b, preferred_element_type=jnp.float32)


def _rms(x, w):
    xf = x.astype(jnp.float32)
    r = lax.rsqrt(jnp.mean(xf * xf, axis=-1, keepdims=True) + EPS)
    return (xf * r * w.astype(jnp.float32)).astype(jnp.bfloat16)


def _rope(x):
    s, half = x.shape[1], x.shape[-1] // 2
    freq = 10000.0 ** (-jnp.arange(half, dtype=jnp.float32) / half)
    ang = jnp.arange(s, dtype=jnp.float32)[:, None] * freq[None, :]
    c = jnp.cos(ang)[None, :, None, :]
    sn = jnp.sin(ang)[None, :, None, :]
    x1, x2 = x[..., :half], x[..., half:]
    return jnp.concatenate([x1 * c - x2 * sn, x2 * c + x1 * sn], axis=-1)


def _dense(h0, ln_attn, wq, wk, wv, wo, ln_ffn, ws1, ws3, ws2):
    b, s, _ = h0.shape
    nh = wq.shape[1] // HEAD
    x1 = _rms(h0, ln_attn)
    q = _rope(_mm('bsd,de->bse', x1, wq).reshape(b, s, nh, HEAD)).astype(jnp.bfloat16)
    k = _rope(_mm('bsd,de->bse', x1, wk).reshape(b, s, nh, HEAD)).astype(jnp.bfloat16)
    v = _mm('bsd,de->bse', x1, wv).astype(jnp.bfloat16).reshape(b, s, nh, HEAD)
    sc = _mm('bqhe,bkhe->bhqk', q, k) * HEAD ** -0.5
    causal = jnp.arange(s)[:, None] >= jnp.arange(s)[None, :]
    p = jax.nn.softmax(jnp.where(causal, sc, -1e30), axis=-1).astype(jnp.bfloat16)
    o = _mm('bhqk,bkhe->bqhe', p, v).astype(jnp.bfloat16).reshape(b, s, nh * HEAD)
    a = (h0.astype(jnp.float32) + _mm('bse,ed->bsd', o, wo)).astype(jnp.bfloat16)
    x2 = _rms(a, ln_ffn)
    hs = (jax.nn.silu(_mm('bsd,df->bsf', x2, ws1)) * _mm('bsd,df->bsf', x2, ws3)).astype(jnp.bfloat16)
    return a, _mm('bsf,fd->bsd', hs, ws2)


def _experts(x, ue1, ue3, ue2):
    he = (jax.nn.silu(_mm('gecd,edf->egcf', x, ue1)) * _mm('gecd,edf->egcf', x, ue3)).astype(jnp.bfloat16)
    return _mm('egcf,efd->gecd', he, ue2).astype(jnp.bfloat16)


def _gate(u, wr, gi):
    lg = _mm('td,de->te', u, wr)
    hit = gi[..., None] == jnp.arange(wr.shape[1], dtype=gi.dtype)
    return jax.nn.softmax(jnp.sum(jnp.where(hit, lg[:, None, :], 0.0), axis=-1), axis=-1)


def _route(q, gate, n):
    hit = q[..., None] == jnp.arange(n, dtype=q.dtype)
    disp = jnp.any(hit, axis=-2).astype(jnp.bfloat16)
    comb = jnp.sum(jnp.where(hit, gate[..., None], 0.0), axis=-2)
    return disp, comb


def _parts(c):
    hi = c.astype(jnp.bfloat16)
    r = c - hi.astype(jnp.float32)
    mid = r.astype(jnp.bfloat16)
    lo = (r - mid.astype(jnp.float32)).astype(jnp.bfloat16)
    return hi, mid, lo


def solution(mesh):
    g_ = mesh.shape['ep']
    rows = P(('dp', 'ep'))
    rep = P()

    def local(h0, idx, slot, ln_attn, wq, wk, wv, wo, ln_ffn, ws1, ws3, ws2, ln_moe, wr, ue1, ue3, ue2):
        b, s, d = h0.shape
        top = idx.shape[-1]
        el = ue1.shape[0]
        ne = el * g_
        t = b * s
        cap = CAP_FACTOR * t * top // ne
        a, fo = _dense(h0, ln_attn, wq, wk, wv, wo, ln_ffn, ws1, ws3, ws2)
        u = _rms(h0, ln_moe).reshape(t, d)
        gi = idx.reshape(t, top)
        sl = slot.reshape(t, top)
        gate = _gate(u, wr, gi)
        disp, comb = _route(gi * cap + sl, gate, ne * cap)
        send = _mm('tr,td->rd', disp, u).astype(jnp.bfloat16).reshape(g_, el, cap, d)
        recv = lax.all_to_all(send, 'ep', 0, 0, tiled=True)
        y = _experts(recv, ue1, ue3, ue2)
        back = lax.all_to_all(y, 'ep', 0, 0, tiled=True).reshape(ne * cap, d)
        m = sum(_mm('tr,rd->td', p, back) for p in _parts(comb))
        out = a.astype(jnp.float32) + fo + m.reshape(b, s, d)
        return out.astype(jnp.bfloat16)

    specs = (rows, rows, rows) + (rep,) * 11 + (P('ep'), P('ep'), P('ep'))
    return jax.shard_map(local, mesh=mesh, in_specs=specs, out_specs=rows, check_vma=False)
```

profile of v0, /device:TPU:0, one launch (start us, length us, event | category | flops | bytes accessed | tf_op | source)
XLA Modules:
  0.0 464.2 jit_solution(9943689774310732269)
XLA Ops:
  0.0 1.6 fusion.28
  1.6 0.7 bitcast_add_fusion
  2.3 0.6 copy-done.3
  2.9 4.2 fusion.7
  7.1 0.7 convert_element_type.103
  7.8 7.8 %convolution_convert_fusion = bf16[3072,2048]{1,0:T(8,128)(2,1)} fusion(pred[256,3072]{1,0:T(8,128)(4,1)S(1)} %fusion.7, bf16[1,256,2048]{2,1,0:T(8,128)(2,1)} %param.17, f32[2048]{0:T(1024)S(1)} %convert_element_type.103, f32[256]{0:T(256)S(1)} %add_rsqrt_fusion.1), kind=kOutput, calls=%fused_computation.12 | convolution fusion | flops 3229614080 | bytes 14427136 | tf_op jit(solution)/shard_map/tr,td->rd/dot_general | solution.py:12
  15.6 6.6 %all-to-all-start = ((bf16[4,16,48,2048]{3,2,1,0:T(8,128)(2,1)}), bf16[4,16,48,2048]{3,2,1,0:T(8,128)(2,1)}, u32[]{:S(2)}, u32[]{:S(2)}) async-start(bf16[4,16,48,2048]{3,2,1,0:T(8,128)(2,1)} %bitcast.100), calls=%async_computation | async-start | bytes 25165824 | tf_op jit(solution)/shard_map/all_to_all | solution.py:93
  22.2 0.6 copy.79
  22.8 138.1 %all-to-all-done = bf16[4,16,48,2048]{3,2,1,0:T(8,128)(2,1)} async-done(((bf16[4,16,48,2048]{3,2,1,0:T(8,128)(2,1)}), bf16[4,16,48,2048]{3,2,1,0:T(8,128)(2,1)}, u32[]{:S(2)}, u32[]{:S(2)}) %all-to-all-start) | async-done | bytes 12582944 | tf_op jit(solution)/shard_map/all_to_all | solution.py:93
  161.0 40.9 %fusion.3 = f32[16,4,48,1408]{3,2,1,0:T(8,128)} fusion(bf16[16,2048,1408]{2,1,0:T(8,128)(2,1)} %param.32, bf16[4,16,48,2048]{3,2,1,0:T(8,128)(2,1)} %all-to-all-done), kind=kOutput, calls=%fused_computation.3 | convolution fusion | flops 17716740096 | bytes 122159104 | tf_op jit(solution)/shard_map/gecd,edf->egcf/dot_general | solution.py:12
  201.8 46.2 %multiply_convert_fusion = bf16[16,4,48,1408]{3,2,1,0:T(8,128)(2,1)} fusion(f32[16,4,48,1408]{3,2,1,0:T(8,128)} %fusion.3, bf16[16,2048,1408]{2,1,0:T(8,128)(2,1)} %param.31, bf16[4,16,48,2048]{3,2,1,0:T(8,128)(2,1)} %all-to-all-done), kind=kOutput, calls=%fused_computation.10 | convolution fusion | flops 17742692352 | bytes 130809856 | tf_op jit(solution)/shard_map/gecd,edf->egcf/dot_general | solution.py:12
  248.1 38.6 %convert_bitcast_fusion = bf16[4,16,48,2048]{3,2,0,1:T(8,128)(2,1)} fusion(bf16[16,4,48,1408]{3,2,1,0:T(8,128)(2,1)} %multiply_convert_fusion, bf16[16,1408,2048]{2,1,0:T(8,128)(2,1)} %param.33), kind=kOutput, calls=%fused_computation.11 | convolution fusion | flops 17723031552 | bytes 113508352 | tf_op jit(solution)/shard_map/egcf,efd->gecd/dot_general | solution.py:12
  286.7 10.7 %copy.59 = bf16[4,16,48,2048]{3,2,1,0:T(8,128)(2,1)} copy(bf16[4,16,48,2048]{3,2,0,1:T(8,128)(2,1)} %convert_bitcast_fusion) | data formatting | bytes 25165824 | tf_op jit(solution)/shard_map/convert_element_type | solution.py:50
  297.4 6.7 %all-to-all-start.1 = ((bf16[4,16,48,2048]{3,2,1,0:T(8,128)(2,1)}), bf16[4,16,48,2048]{3,2,1,0:T(8,128)(2,1)}, u32[]{:S(2)}, u32[]{:S(2)}) async-start(bf16[4,16,48,2048]{3,2,1,0:T(8,128)(2,1)} %copy.59), calls=%async_computation.1 | async-start | bytes 25165824 | tf_op jit(solution)/shard_map/all_to_all | solution.py:95
  304.1 5.8 %convolution_convert_fusion.1 = bf16[256,2048]{1,0:T(8,128)(2,1)S(1)} fusion(bf16[2048,2048]{1,0:T(8,128)(2,1)} %param.23, bf16[1,256,2048]{2,1,0:T(8,128)(2,1)S(1)} %copy-done.1, f32[2048]{0:T(1024)S(1)} %convert_element_type.91, f32[256]{0:T(256)S(1)} %add_rsqrt_fusion.1), kind=kOutput, calls=%fused_computation.37 | convolution fusion | flops 2150105088 | bytes 10494976 | tf_op jit(solution)/shard_map/bsd,de->bse/dot_general | solution.py:12
  310.4 12.4 %copy.68 = bf16[2048,2048]{1,0:T(8,128)(2,1)} copy(bf16[2048,2048]{0,1:T(8,128)(2,1)} %bitcast.103) | data formatting | bytes 16777216 | tf_op jit(solution)/shard_map/bsd,de->bse/dot_general | solution.py:12
  322.8 12.3 %copy.67 = bf16[2048,2048]{1,0:T(8,128)(2,1)} copy(bf16[2048,2048]{0,1:T(8,128)(2,1)} %bitcast.104) | data formatting | bytes 16777216 | tf_op jit(solution)/shard_map/bsd,de->bse/dot_general | solution.py:12
  336.1 5.8 %convolution_bitcast_fusion.2 = f32[1,256,16,128]{1,3,2,0:T(8,128)S(1)} fusion(bf16[16,128,2048]{2,1,0:T(8,128)(2,1)} %bitcast.106, bf16[1,256,2048]{2,1,0:T(8,128)(2,1)S(1)} %copy-done.1, f32[2048]{0:T(1024)S(1)} %convert_element_type.91, f32[256]{0:T(256)S(1)} %add_rsqrt_fusion.1), kind=kOutput, calls=%fused_computation.53 | convolution fusion | flops 2149580800 | bytes 11543552 | tf_op jit(solution)/shard_map/bsd,de->bse/dot_general | solution.py:12
  342.0 5.8 %convolution_bitcast_fusion.3 = f32[1,256,16,128]{1,3,2,0:T(8,128)S(1)} fusion(bf16[16,128,2048]{2,1,0:T(8,128)(2,1)} %bitcast.105, bf16[1,256,2048]{2,1,0:T(8,128)(2,1)S(1)} %copy-done.1, f32[2048]{0:T(1024)S(1)} %convert_element_type.91, f32[256]{0:T(256)S(1)} %add_rsqrt_fusion.1), kind=kOutput, calls=%fused_computation.54 | convolution fusion | flops 2149580800 | bytes 11543552 | tf_op jit(solution)/shard_map/bsd,de->bse/dot_general | solution.py:12
  347.8 0.7 fusion.51
  348.5 0.8 fusion.39
  349.3 1.7 fusion.71
  351.0 0.5 fusion.36
  351.5 1.7 slice-done.1
  353.3 2.5 fusion.29
  355.8 4.2 select_reduce_fusion
  360.0 4.9 %fusion.55 = f32[256,2816]{1,0:T(8,128)} fusion(bf16[2048,2816]{1,0:T(8,128)(2,1)S(1)} %bitcast.111, bf16[1,256,2048]{2,1,0:T(8,128)(2,1)S(1)} %get-tuple-element.16, f32[2048]{0:T(1024)S(1)} %convert_element_type.100, f32[256]{0:T(256)S(1)} %add_rsqrt_fusion), kind=kOutput, calls=%fused_computation.78 | convolution fusion | flops 2954887168 | bytes 15475712 | tf_op jit(solution)/shard_map/bsd,df->bsf/dot_general | solution.py:12
  364.9 16.8 %convert_add_fusion = f32[1,256,2048]{2,1,0:T(8,128)} fusion(bf16[1,256,2048]{2,1,0:T(8,128)(2,1)} %copy-done.2, bf16[2816,2048]{1,0:T(8,128)(2,1)} %param.28, bf16[2048,2816]{1,0:T(8,128)(2,1)} %param.27, f32[256,2816]{1,0:T(8,128)} %fusion.55, f32[2048]{0:T(1024)S(1)} %convert_element_type.100, f32[256]{0:T(256)S(1)} %add_rsqrt_fusion), kind=kOutput, calls=%fused_computation.23 | convolution fusion | flops 5913051136 | bytes 29107200 | tf_op jit(solution)/shard_map/bsf,fd->bsd/dot_general | solution.py:12
  381.7 60.1 %all-to-all-done.1 = bf16[4,16,48,2048]{3,2,1,0:T(8,128)(2,1)} async-done(((bf16[4,16,48,2048]{3,2,1,0:T(8,128)(2,1)}), bf16[4,16,48,2048]{3,2,1,0:T(8,128)(2,1)}, u32[]{:S(2)}, u32[]{:S(2)}) %all-to-all-start.1) | async-done | bytes 12582944 | tf_op jit(solution)/shard_map/all_to_all | solution.py:95
  441.9 6.4 %fusion.23 = f32[256,2048]{1,0:T(8,128)S(1)} fusion(bf16[3072,2048]{1,0:T(8,128)(2,1)} %bitcast.28, f32[256,3072]{1,0:T(8,128)S(1)} %select_reduce_fusion), kind=kOutput, calls=%fused_computation.41 | convolution fusion | flops 3222011904 | bytes 17825792 | tf_op jit(solution)/shard_map/tr,rd->td/dot_general | solution.py:12
  448.3 6.6 %convolution_add_fusion.1 = f32[256,2048]{1,0:T(8,128)S(1)} fusion(f32[256,2048]{1,0:T(8,128)S(1)} %fusion.23, bf16[3072,2048]{1,0:T(8,128)(2,1)} %bitcast.28, f32[256,3072]{1,0:T(8,128)S(1)} %select_reduce_fusion), kind=kOutput, calls=%fused_computation.34 | convolution fusion | flops 3224895488 | bytes 19922944 | tf_op jit(solution)/shard_map/tr,rd->td/dot_general | solution.py:12
  454.9 9.1 %fusion.18 = bf16[1,256,2048]{2,1,0:T(8,128)(2,1)} fusion(f32[1,256,2048]{2,1,0:T(8,128)S(1)} %copy-done.11, f32[256,2048]{1,0:T(8,128)S(1)} %convolution_add_fusion.1, bf16[3072,2048]{1,0:T(8,128)(2,1)} %bitcast.28, f32[256,3072]{1,0:T(8,128)S(1)} %select_reduce_fusion), kind=kOutput, calls=%fused_computation.35 | convolution fusion | flops 3228303360 | bytes 20971520 | tf_op jit(solution)/shard_map/tr,rd->td/dot_general | solution.py:12
  (47 shorter events, 1.6 us)
Async XLA Ops:
  0.0 335.1 %copy-start = (bf16[2048,64]{0,1:T(8,128)(2,1)S(1)}, bf16[2048,64]{0,1:T(8,128)(2,1)}, u32[]{:S(2)}) copy-start(bf16[2048,64]{0,1:T(8,128)(2,1)} %param.30) | copy-start | bytes 786436
  2.3 0.6 copy-start.3
  7.8 7.8 %copy-start.5 = (f32[2048]{0:T(1024)}, f32[2048]{0:T(1024)S(1)}, u32[]{:S(2)}) copy-start(f32[2048]{0:T(1024)S(1)} %convert_element_type.103) | copy-start | bytes 24580
  15.6 6.6 %copy-start.8 = (s32[1,256,6]{1,0,2:T(1,128)S(1)}, s32[1,256,6]{1,0,2:T(1,128)}, u32[]{:S(2)}) copy-start(s32[1,256,6]{1,0,2:T(1,128)} %param.18) | copy-start | bytes 18436
  15.6 7.2 %copy-start.9 = (bf16[2048]{0:T(1024)(128)(2,1)S(1)}, bf16[2048]{0:T(1024)(128)(2,1)}, u32[]{:S(2)}) copy-start(bf16[2048]{0:T(1024)(128)(2,1)} %param.20) | copy-start | bytes 12292
  15.6 145.4 %all-to-all-start = ((bf16[4,16,48,2048]{3,2,1,0:T(8,128)(2,1)}), bf16[4,16,48,2048]{3,2,1,0:T(8,128)(2,1)}, u32[]{:S(2)}, u32[]{:S(2)}) async-start(bf16[4,16,48,2048]{3,2,1,0:T(8,128)(2,1)} %bitcast.100), calls=%async_computation | async-start | bytes 25165824 | tf_op jit(solution)/shard_map/all_to_all | solution.py:93
  297.4 6.7 %copy-start.1 = (bf16[1,256,2048]{2,1,0:T(8,128)(2,1)S(1)}, bf16[1,256,2048]{2,1,0:T(8,128)(2,1)}, u32[]{:S(2)}) copy-start(bf16[1,256,2048]{2,1,0:T(8,128)(2,1)} %param.17) | copy-start | bytes 3145732
  297.4 144.4 %all-to-all-start.1 = ((bf16[4,16,48,2048]{3,2,1,0:T(8,128)(2,1)}), bf16[4,16,48,2048]{3,2,1,0:T(8,128)(2,1)}, u32[]{:S(2)}, u32[]{:S(2)}) async-start(bf16[4,16,48,2048]{3,2,1,0:T(8,128)(2,1)} %copy.59), calls=%async_computation.1 | async-start | bytes 25165824 | tf_op jit(solution)/shard_map/all_to_all | solution.py:95
  322.8 12.3 %copy-start.10 = (bf16[2048]{0:T(1024)(128)(2,1)S(1)}, bf16[2048]{0:T(1024)(128)(2,1)}, u32[]{:S(2)}) copy-start(bf16[2048]{0:T(1024)(128)(2,1)} %param.25) | copy-start | bytes 12292
  322.8 12.3 %copy-start.6 = (f32[2048]{0:T(1024)S(1)}, f32[2048]{0:T(1024)}, u32[]{:S(2)}) copy-start(f32[2048]{0:T(1024)} %copy-done.5) | copy-start | bytes 24580
  322.8 12.8 %copy-start.7 = (s32[1,256,6]{1,2,0:T(8,128)S(1)}, s32[1,256,6]{1,2,0:T(8,128)}, u32[]{:S(2)}) copy-start(s32[1,256,6]{1,2,0:T(8,128)} %copy.79) | copy-start | bytes 18436
  349.3 2.3 slice-start
  350.9 2.3 slice-start.1
  351.0 9.0 %slice-start.2 = ((s8[11534336]{0:T(1024)(128)(4,1)}), s8[4194304]{0:T(1024)(128)(4,1)S(1)}, s32[]{:S(2)}) async-start(s8[11534336]{0:T(1024)(128)(4,1)} %bitcast.110), calls=%async_computation.4 | async-start | bytes 8388608
  351.0 9.0 %slice-start.3 = ((s8[11534336]{0:T(1024)(128)(4,1)}), s8[4194304]{0:T(1024)(128)(4,1)S(1)}, s32[]{:S(2)}) async-start(s8[11534336]{0:T(1024)(128)(4,1)} %bitcast.110), calls=%async_computation.5 | async-start | bytes 8388608
  353.3 2.5 copy-start.4
  353.3 6.7 %slice-start.4 = ((s8[11534336]{0:T(1024)(128)(4,1)}), s8[3145728]{0:T(1024)(128)(4,1)S(1)}, s32[]{:S(2)}) async-start(s8[11534336]{0:T(1024)(128)(4,1)} %bitcast.110), calls=%async_computation.6 | async-start | bytes 6291456
  355.8 4.2 copy-start.2
  448.3 6.6 %copy-start.11 = (f32[1,256,2048]{2,1,0:T(8,128)S(1)}, f32[1,256,2048]{2,1,0:T(8,128)}, u32[]{:S(2)}) copy-start(f32[1,256,2048]{2,1,0:T(8,128)} %convert_add_fusion) | copy-start | bytes 6291460
where the time goes:
time: 471 us; the launch traced here: 464 us
  matrix products  199 us (42%)
  waiting for transfers between devices  198 us (42%)
  local copies, waits for them, and re-layouts  38.9 us (8%)
  other arithmetic  14.1 us (3%)
  starting transfers between devices  13.3 us (3%)
    dot_general x16, matrix products, _mm(): return jnp.einsum(form, a, b, preferred_element_type=jnp.float32)  199 us
    all_to_all x1, waiting for transfers between devices, local(): recv = lax.all_to_all(send, 'ep', 0, 0, tiled=True)  138 us
    all_to_all x1, waiting for transfers between devices, local(): back = lax.all_to_all(y, 'ep', 0, 0, tiled=True).reshape(ne * cap, d)  60.1 us
    dot_general x2, local copies, waits for them, and re-layouts, _mm(): return jnp.einsum(form, a, b, preferred_element_type=jnp.float32)  24.7 us
    convert_element_type x1, local copies, waits for them, and re-layouts, _experts(): return _mm('egcf,efd->gecd', he, ue2).astype(jnp.bfloat16)  10.7 us
  transfers between devices with their start and end apart: 2, of which 2 were waited for; matrix products, arithmetic and copies ran while one was open for 16% of the time, Pallas kernels for 0%

commit v1 on v0

--- a/solution.py
+++ b/solution.py
@@ -56,13 +56,6 @@
     return jax.nn.softmax(jnp.sum(jnp.where(hit, lg[:, None, :], 0.0), axis=-1), axis=-1)
 
 
-def _route(q, gate, n):
-    hit = q[..., None] == jnp.arange(n, dtype=q.dtype)
-    disp = jnp.any(hit, axis=-2).astype(jnp.bfloat16)
-    comb = jnp.sum(jnp.where(hit, gate[..., None], 0.0), axis=-2)
-    return disp, comb
-
-
 def _parts(c):
     hi = c.astype(jnp.bfloat16)
     r = c - hi.astype(jnp.float32)
@@ -72,29 +65,38 @@
 
 
 def solution(mesh):
-    g_ = mesh.shape['ep']
     rows = P(('dp', 'ep'))
     rep = P()
+    core = [(k, k ^ 1) for k in range(4)]
+    chip = [(k, k ^ 2) for k in range(4)]
 
     def local(h0, idx, slot, ln_attn, wq, wk, wv, wo, ln_ffn, ws1, ws3, ws2, ln_moe, wr, ue1, ue3, ue2):
         b, s, d = h0.shape
         top = idx.shape[-1]
         el = ue1.shape[0]
-        ne = el * g_
         t = b * s
-        cap = CAP_FACTOR * t * top // ne
-        a, fo = _dense(h0, ln_attn, wq, wk, wv, wo, ln_ffn, ws1, ws3, ws2)
+        cap = CAP_FACTOR * t * top // (el * mesh.shape['ep'])
         u = _rms(h0, ln_moe).reshape(t, d)
         gi = idx.reshape(t, top)
-        sl = slot.reshape(t, top)
         gate = _gate(u, wr, gi)
-        disp, comb = _route(gi * cap + sl, gate, ne * cap)
-        send = _mm('tr,td->rd', disp, u).astype(jnp.bfloat16).reshape(g_, el, cap, d)
-        recv = lax.all_to_all(send, 'ep', 0, 0, tiled=True)
-        y = _experts(recv, ue1, ue3, ue2)
-        back = lax.all_to_all(y, 'ep', 0, 0, tiled=True).reshape(ne * cap, d)
-        m = sum(_mm('tr,rd->td', p, back) for p in _parts(comb))
-        out = a.astype(jnp.float32) + fo + m.reshape(b, s, d)
+        pos = (gi * cap + slot.reshape(t, top)).astype(jnp.float32)
+        pk = jnp.concatenate([pos, gate], axis=-1)
+        ux, kx = lax.ppermute(u, 'ep', chip), lax.ppermute(pk, 'ep', chip)
+        uc, kc = lax.ppermute(u, 'ep', core), lax.ppermute(pk, 'ep', core)
+        uxc, kxc = lax.ppermute(ux, 'ep', core), lax.ppermute(kx, 'ep', core)
+        a, fo = _dense(h0, ln_attn, wq, wk, wv, wo, ln_ffn, ws1, ws3, ws2)
+        us = jnp.stack([u, uc, ux, uxc])
+        ks = jnp.stack([pk, kc, kx, kxc])
+        ps = ks[..., :top].astype(jnp.int32) - lax.axis_index('ep') * (el * cap)
+        hit = ps[..., None] == jnp.arange(el * cap, dtype=jnp.int32)
+        disp = jnp.any(hit, axis=-2).astype(jnp.bfloat16)
+        comb = jnp.sum(jnp.where(hit, ks[..., top:, None], 0.0), axis=-2)
+        x = _mm('gtr,gtd->grd', disp, us).astype(jnp.bfloat16).reshape(4, el, cap, d)
+        y = _experts(x, ue1, ue3, ue2).reshape(4, el * cap, d)
+        m = sum(_mm('gtr,grd->gtd', p, y) for p in _parts(comb))
+        got = lax.ppermute(jnp.stack([m[1], m[3]]), 'ep', core)
+        far = lax.ppermute(m[2] + got[1], 'ep', chip)
+        out = a.astype(jnp.float32) + fo + (m[0] + got[0] + far).reshape(b, s, d)
         return out.astype(jnp.bfloat16)
 
     specs = (rows, rows, rows) + (rep,) * 11 + (P('ep'), P('ep'), P('ep'))

time: 471 us -> 299 us (0.63)
  waiting for transfers between devices: 198 us -> 25.3 us
  other arithmetic: 14.1 us -> 22.2 us
  starting transfers between devices: 13.3 us -> 6.18 us
    all_to_all x2 -> x0, waiting for transfers between devices: 198 us -> none  [the longest x1 138 us: local(): recv = lax.all_to_all(send, 'ep', 0, 0, tiled=True)]
    ppermute x0 -> x8, waiting for transfers between devices: none -> 25.3 us  [the longest x1 25.3 us: local(): far = lax.ppermute(m[2] + got[1], 'ep', chip)]
    all_to_all x2 -> x0, starting transfers between devices: 13.3 us -> none  [the longest x1 6.66 us: local(): back = lax.all_to_all(y, 'ep', 0, 0, tiled=True).reshape(ne * cap, d)]
    ppermute x0 -> x8, starting transfers between devices: none -> 6.18 us  [the longest x2 3.34 us: local(): ux, kx = (lax.ppermute(u, 'ep', chip), lax.ppermute(pk, 'ep', chip))]
    convert_element_type x0 -> x2, other arithmetic: none -> 5.12 us  [the longest x1 5.11 us: local(): return out.astype(jnp.bfloat16)]
  transfers between devices with their start and end apart: 2 -> 8, of which waited for: 2 -> 1; matrix products, arithmetic and copies ran while one was open for 16% -> 26% of each run, Pallas kernels for 0% -> 0%
where the time goes in v1:
time: 299 us; the launch traced here: 295 us
  matrix products  199 us (67%)
  local copies, waits for them, and re-layouts  42 us (14%)
  waiting for transfers between devices  25.3 us (8%)
  other arithmetic  22.2 us (7%)
  starting transfers between devices  6.18 us (2%)
    dot_general x16, matrix products, _mm(): return jnp.einsum(form, a, b, preferred_element_type=jnp.float32)  199 us
    ppermute x1, waiting for transfers between devices, local(): far = lax.ppermute(m[2] + got[1], 'ep', chip)  25.3 us
    dot_general x2, local copies, waits for them, and re-layouts, _mm(): return jnp.einsum(form, a, b, preferred_element_type=jnp.float32)  25 us
    unnamed x53, local copies, waits for them, and re-layouts  6.76 us
    convert_element_type x1, local copies, waits for them, and re-layouts, _experts(): return _mm('egcf,efd->gecd', he, ue2).astype(jnp.bfloat16)  6.45 us
  transfers between devices with their start and end apart: 8, of which 1 were waited for; matrix products, arithmetic and copies ran while one was open for 26% of the time, Pallas kernels for 0%

profile of v1, /device:TPU:0, one launch (start us, length us, event | category | flops | bytes accessed | tf_op | source)
XLA Modules:
  0.0 295.2 jit_solution(13812480637226816246)
XLA Ops:
  0.0 1.6 fusion.33
  3.0 1.5 fusion.32
  6.2 3.3 %collective-permute-start.1 = (f32[256,12]{0,1:T(8,128)S(1)}, f32[256,12]{0,1:T(8,128)S(1)}, u32[]{:S(2)}, u32[]{:S(2)}) collective-permute-start(f32[256,12]{0,1:T(8,128)S(1)} %get-tuple-element.14), channel_id=1, source_target_pairs={{0,2},{1,3},{2,0},{3,1},{4,6},{5,7},{6,4},{7,5},{8,10},{9,11},{10,... | collective-permute-start | bytes 36872 | tf_op jit(solution)/shard_map/ppermute | solution.py:84
  9.5 1.3 fusion.101
  11.3 5.8 %convolution_convert_fusion.1 = bf16[256,2048]{1,0:T(8,128)(2,1)S(1)} fusion(bf16[2048,2048]{1,0:T(8,128)(2,1)} %param.23, bf16[1,256,2048]{2,1,0:T(8,128)(2,1)S(1)} %copy-done.3, f32[2048]{0:T(1024)S(1)} %convert_element_type.97, f32[256]{0:T(256)S(1)} %add_rsqrt_fusion.1), kind=kOutput, calls=%fused_computation.41 | convolution fusion | flops 2150105088 | bytes 10494976 | tf_op jit(solution)/shard_map/bsd,de->bse/dot_general | solution.py:12
  17.2 1.0 fusion.68
  18.2 12.6 %copy.60 = bf16[2048,2048]{1,0:T(8,128)(2,1)} copy(bf16[2048,2048]{0,1:T(8,128)(2,1)} %bitcast.127) | data formatting | bytes 16777216 | tf_op jit(solution)/shard_map/bsd,de->bse/dot_general | solution.py:12
  30.8 12.4 %copy.59 = bf16[2048,2048]{1,0:T(8,128)(2,1)} copy(bf16[2048,2048]{0,1:T(8,128)(2,1)} %bitcast.128) | data formatting | bytes 16777216 | tf_op jit(solution)/shard_map/bsd,de->bse/dot_general | solution.py:12
  43.1 1.3 copy.58
  45.6 3.1 %fusion.7 = pred[4,256,768]{2,1,0:T(8,128)(4,1)S(1)} fusion(s32[4,256,6]{1,2,0:T(8,128)S(1)} %fusion.69), kind=kLoop, calls=%fused_computation.9 | loop fusion | flops 8650752 | bytes 811008 | tf_op jit(solution)/shard_map/reduce_or | solution.py:92
  48.7 2.7 select_reduce_fusion
  51.4 7.8 %convolution_convert_fusion = bf16[4,768,2048]{2,1,0:T(8,128)(2,1)} fusion(pred[4,256,768]{2,1,0:T(8,128)(4,1)S(1)} %fusion.7, bf16[1,256,2048]{2,1,0:T(8,128)(2,1)S(1)} %bitcast.141, bf16[1,256,2048]{2,1,0:T(8,128)(2,1)} %bitcast.25, bf16[1,256,2048]{2,1,0:T(8,128)(2,1)} %bitcast.24, bf16[1,256,2048]{2,1,0:T(8,128)(2,1)} %copy-done.6), kind=kOutput, calls=%fused_computation.15 | convolution fusion | flops 3233808384 | bytes 17563648 | tf_op jit(solution)/shard_map/gtr,gtd->grd/dot_general | solution.py:12
  59.2 40.5 %fusion.3 = f32[16,4,48,1408]{3,2,1,0:T(8,128)} fusion(bf16[16,2048,1408]{2,1,0:T(8,128)(2,1)} %param.32, bf16[4,16,48,2048]{3,2,1,0:T(8,128)(2,1)} %bitcast.142), kind=kOutput, calls=%fused_computation.3 | convolution fusion | flops 17716740096 | bytes 122159104 | tf_op jit(solution)/shard_map/gecd,edf->egcf/dot_general | solution.py:12
  99.7 46.2 %multiply_convert_fusion = bf16[16,4,48,1408]{3,2,1,0:T(8,128)(2,1)} fusion(f32[16,4,48,1408]{3,2,1,0:T(8,128)} %fusion.3, bf16[16,2048,1408]{2,1,0:T(8,128)(2,1)} %param.31, bf16[4,16,48,2048]{3,2,1,0:T(8,128)(2,1)} %bitcast.143), kind=kOutput, calls=%fused_computation.10 | convolution fusion | flops 17742692352 | bytes 130809856 | tf_op jit(solution)/shard_map/gecd,edf->egcf/dot_general | solution.py:12
  145.9 39.1 %convert_bitcast_fusion = bf16[4,16,48,2048]{3,2,0,1:T(8,128)(2,1)} fusion(bf16[16,4,48,1408]{3,2,1,0:T(8,128)(2,1)} %multiply_convert_fusion, bf16[16,1408,2048]{2,1,0:T(8,128)(2,1)} %param.33), kind=kOutput, calls=%fused_computation.11 | convolution fusion | flops 17723031552 | bytes 113508352 | tf_op jit(solution)/shard_map/egcf,efd->gecd/dot_general | solution.py:12
  185.0 6.4 %copy.50 = bf16[4,16,48,2048]{3,2,1,0:T(8,128)(2,1)S(1)} copy(bf16[4,16,48,2048]{3,2,0,1:T(8,128)(2,1)} %convert_bitcast_fusion) | data formatting | bytes 25165824 | tf_op jit(solution)/shard_map/convert_element_type | solution.py:50
  191.5 6.5 %fusion.29 = f32[4,256,2048]{2,1,0:T(8,128)} fusion(bf16[4,768,2048]{2,1,0:T(8,128)(2,1)S(1)} %bitcast.122, f32[4,256,768]{2,1,0:T(8,128)S(1)} %select_reduce_fusion), kind=kOutput, calls=%fused_computation.47 | convolution fusion | flops 3224371200 | bytes 24117248 | tf_op jit(solution)/shard_map/gtr,grd->gtd/dot_general | solution.py:12
  198.5 5.7 %fusion.27 = f32[4,256,2048]{2,1,0:T(8,128)} fusion(bf16[4,768,2048]{2,1,0:T(8,128)(2,1)S(1)} %bitcast.123, f32[4,256,768]{2,1,0:T(8,128)S(1)} %select_reduce_fusion), kind=kOutput, calls=%fused_computation.45 | convolution fusion | flops 3222011904 | bytes 24117248 | tf_op jit(solution)/shard_map/gtr,grd->gtd/dot_general | solution.py:12
  204.2 13.5 %add_add_fusion = f32[4,256,2048]{2,1,0:T(8,128)} fusion(f32[4,256,2048]{2,1,0:T(8,128)} %fusion.27, f32[4,256,2048]{2,1,0:T(8,128)} %fusion.29, bf16[4,768,2048]{2,1,0:T(8,128)(2,1)} %bitcast.124, f32[4,256,768]{2,1,0:T(8,128)S(1)} %select_reduce_fusion), kind=kOutput, calls=%fused_computation.14 | convolution fusion | flops 3230924800 | bytes 40894464 | tf_op jit(solution)/shard_map/gtr,grd->gtd/dot_general | solution.py:12
  217.8 2.5 fusion.84
  221.5 6.2 %convolution_bitcast_fusion.2 = f32[1,256,16,128]{1,3,2,0:T(8,128)S(1)} fusion(bf16[16,128,2048]{2,1,0:T(8,128)(2,1)} %bitcast.132, bf16[1,256,2048]{2,1,0:T(8,128)(2,1)S(1)} %copy-done.4, f32[2048]{0:T(1024)S(1)} %copy-done.15, f32[256]{0:T(256)S(1)} %copy-done.12), kind=kOutput, calls=%fused_computation.66 | convolution fusion | flops 2149580800 | bytes 11543552 | tf_op jit(solution)/shard_map/bsd,de->bse/dot_general | solution.py:12
  227.7 2.5 convolution_bitcast_fusion.3
  231.7 1.5 fusion.85
  234.2 1.5 slice-done.1
  235.7 2.5 fusion.34
  238.2 1.9 copy-done.5
  240.1 1.8 fusion.37
  242.0 1.7 collective-permute-start.7
  243.8 4.8 %fusion.65 = f32[256,2816]{1,0:T(8,128)} fusion(bf16[2048,2816]{1,0:T(8,128)(2,1)S(1)} %bitcast.140, bf16[1,256,2048]{2,1,0:T(8,128)(2,1)S(1)} %get-tuple-element.20, f32[2048]{0:T(1024)S(1)} %copy-done.13, f32[256]{0:T(256)S(1)} %add_rsqrt_fusion), kind=kOutput, calls=%fused_computation.90 | convolution fusion | flops 2954887168 | bytes 15475712 | tf_op jit(solution)/shard_map/bsd,df->bsf/dot_general | solution.py:12
  248.6 16.0 %convert_add_fusion = f32[1,256,2048]{2,1,0:T(8,128)} fusion(bf16[1,256,2048]{2,1,0:T(8,128)(2,1)S(1)} %get-tuple-element.20, bf16[2816,2048]{1,0:T(8,128)(2,1)} %param.28, bf16[2048,2816]{1,0:T(8,128)(2,1)} %param.27, f32[256,2816]{1,0:T(8,128)} %fusion.65, f32[2048]{0:T(1024)S(1)} %copy-done.13, f32[256]{0:T(256)S(1)} %add_rsqrt_fusion), kind=kOutput, calls=%fused_computation.32 | convolution fusion | flops 5913051136 | bytes 29107200 | tf_op jit(solution)/shard_map/bsf,fd->bsd/dot_general | solution.py:12
  264.6 25.3 %collective-permute-done.7 = f32[256,2048]{1,0:T(8,128)} collective-permute-done((f32[256,2048]{1,0:T(8,128)S(1)}, f32[256,2048]{1,0:T(8,128)}, u32[]{:S(2)}, u32[]{:S(2)}) %collective-permute-start.7) | collective-permute-done | bytes 2097184 | tf_op jit(solution)/shard_map/ppermute | solution.py:98
  289.9 5.1 %fusion.42 = bf16[1,256,2048]{2,1,0:T(8,128)(2,1)} fusion(f32[1,256,2048]{2,1,0:T(8,128)} %convert_add_fusion, f32[256,2048]{1,0:T(8,128)} %collective-permute-done.7, f32[2,256,2048]{2,1,0:T(8,128)} %copy-done.5, f32[4,256,2048]{2,1,0:T(8,128)} %add_add_fusion), kind=kLoop, calls=%fused_computation.61 | loop fusion | flops 2097152 | bytes 9437184 | tf_op jit(solution)/shard_map/convert_element_type | solution.py:100
  (88 shorter events, 8.9 us)
Async XLA Ops:
  0.0 5.5 %copy-start = (bf16[2048,64]{0,1:T(8,128)(2,1)S(1)}, bf16[2048,64]{0,1:T(8,128)(2,1)}, u32[]{:S(2)}) copy-start(bf16[2048,64]{0,1:T(8,128)(2,1)} %param.30) | copy-start | bytes 786436
  0.0 9.4 %copy-start.3 = (bf16[1,256,2048]{2,1,0:T(8,128)(2,1)S(1)}, bf16[1,256,2048]{2,1,0:T(8,128)(2,1)}, u32[]{:S(2)}) copy-start(bf16[1,256,2048]{2,1,0:T(8,128)(2,1)} %param.17) | copy-start | bytes 3145732
  0.0 6.1 %copy-start.10 = (s32[1,256,6]{1,0,2:T(1,128)S(1)}, s32[1,256,6]{1,0,2:T(1,128)}, u32[]{:S(2)}) copy-start(s32[1,256,6]{1,0,2:T(1,128)} %param.18) | copy-start | bytes 18436
  0.0 6.1 %copy-start.16 = (s32[1,256,6]{1,0,2:T(1,128)S(1)}, s32[1,256,6]{1,0,2:T(1,128)}, u32[]{:S(2)}) copy-start(s32[1,256,6]{1,0,2:T(1,128)} %param.19) | copy-start | bytes 18436
  0.0 11.3 %copy-start.17 = (bf16[2048]{0:T(1024)(128)(2,1)S(1)}, bf16[2048]{0:T(1024)(128)(2,1)}, u32[]{:S(2)}) copy-start(bf16[2048]{0:T(1024)(128)(2,1)} %param.20) | copy-start | bytes 12292
  1.6 15.4 %copy-start.11 = (f32[256]{0:T(256)}, f32[256]{0:T(256)S(1)}, u32[]{:S(2)}) copy-start(f32[256]{0:T(256)S(1)} %add_rsqrt_fusion.1) | copy-start | bytes 3076
  6.2 10.9 %collective-permute-start.1 = (f32[256,12]{0,1:T(8,128)S(1)}, f32[256,12]{0,1:T(8,128)S(1)}, u32[]{:S(2)}, u32[]{:S(2)}) collective-permute-start(f32[256,12]{0,1:T(8,128)S(1)} %get-tuple-element.14), channel_id=1, source_target_pairs={{0,2},{1,3},{2,0},{3,1},{4,6},{5,7},{6,4},{7,5},{8,10},{9,11},{10,... | collective-permute-start | bytes 36872 | tf_op jit(solution)/shard_map/ppermute | solution.py:84
  9.4 35.6 %collective-permute-start = (f32[256,12]{0,1:T(8,128)S(1)}, f32[256,12]{0,1:T(8,128)S(1)}, u32[]{:S(2)}, u32[]{:S(2)}) collective-permute-start(f32[256,12]{0,1:T(8,128)S(1)} %get-tuple-element.14), channel_id=1, source_target_pairs={{0,1},{1,0},{2,3},{3,2},{4,5},{5,4},{6,7},{7,6},{8,9},{9,8},{10,11... | collective-permute-start | bytes 36872 | tf_op jit(solution)/shard_map/ppermute | solution.py:85
  10.8 34.3 %collective-permute-start.4 = (bf16[256,2048]{1,0:T(8,128)(2,1)}, bf16[256,2048]{1,0:T(8,128)(2,1)}, u32[]{:S(2)}, u32[]{:S(2)}) collective-permute-start(bf16[256,2048]{1,0:T(8,128)(2,1)} %fusion.101), channel_id=1, source_target_pairs={{0,2},{1,3},{2,0},{3,1},{4,6},{5,7},{6,4},{7,5},{8,10},{9,11},{10,... | collective-permute-start | bytes 3145736 | tf_op jit(solution)/shard_map/ppermute | solution.py:84
  10.8 40.5 %collective-permute-start.3 = (bf16[256,2048]{1,0:T(8,128)(2,1)}, bf16[256,2048]{1,0:T(8,128)(2,1)}, u32[]{:S(2)}, u32[]{:S(2)}) collective-permute-start(bf16[256,2048]{1,0:T(8,128)(2,1)} %fusion.101), channel_id=1, source_target_pairs={{0,1},{1,0},{2,3},{3,2},{4,5},{5,4},{6,7},{7,6},{8,9},{9,8},{10,11... | collective-permute-start | bytes 3145736 | tf_op jit(solution)/shard_map/ppermute | solution.py:85
  11.3 5.8 %copy-start.14 = (f32[2048]{0:T(1024)}, f32[2048]{0:T(1024)S(1)}, u32[]{:S(2)}) copy-start(f32[2048]{0:T(1024)S(1)} %convert_element_type.97) | copy-start | bytes 24580
  17.1 28.0 %collective-permute-start.2 = (f32[256,12]{0,1:T(8,128)S(1)}, f32[256,12]{0,1:T(8,128)S(1)}, u32[]{:S(2)}, u32[]{:S(2)}) collective-permute-start(f32[256,12]{0,1:T(8,128)S(1)} %collective-permute-done.1), channel_id=1, source_target_pairs={{0,1},{1,0},{2,3},{3,2},{4,5},{5,4},{6,7},{7,6},{8,9},{9,8},{10,11... | collective-permute-start | bytes 36872 | tf_op jit(solution)/shard_map/ppermute | solution.py:86
  30.8 13.7 %copy-start.18 = (bf16[2048]{0:T(1024)(128)(2,1)S(1)}, bf16[2048]{0:T(1024)(128)(2,1)}, u32[]{:S(2)}) copy-start(bf16[2048]{0:T(1024)(128)(2,1)} %param.25) | copy-start | bytes 12292
  45.1 6.3 %collective-permute-start.5 = (bf16[256,2048]{1,0:T(8,128)(2,1)}, bf16[256,2048]{1,0:T(8,128)(2,1)S(1)}, u32[]{:S(2)}, u32[]{:S(2)}) collective-permute-start(bf16[256,2048]{1,0:T(8,128)(2,1)} %collective-permute-done.4), channel_id=1, source_target_pairs={{0,1},{1,0},{2,3},{3,2},{4,5},{5,4},{6,7},{7,6},{8,9},{9,8},{10,11... | collective-permute-start | bytes 3145736 | tf_op jit(solution)/shard_map/ppermute | solution.py:86
  191.5 7.0 %copy-start.2 = (bf16[4,16,48,2048]{3,2,1,0:T(8,128)(2,1)}, bf16[4,16,48,2048]{3,2,1,0:T(8,128)(2,1)S(1)}, u32[]{:S(2)}) copy-start(bf16[4,16,48,2048]{3,2,1,0:T(8,128)(2,1)S(1)} %copy.50) | copy-start | bytes 37748740
  220.3 1.2 copy-start.4
  220.3 1.2 copy-start.12
  220.3 7.4 %slice-start.2 = ((s8[8388608]{0:T(1024)(128)(4,1)}), s8[4194304]{0:T(1024)(128)(4,1)S(1)}, s32[]{:S(2)}) async-start(s8[8388608]{0:T(1024)(128)(4,1)} %bitcast.129), calls=%async_computation.2 | async-start | bytes 8388608
  220.8 17.4 %collective-permute-start.6 = (f32[2,256,2048]{2,1,0:T(8,128)S(1)}, f32[2,256,2048]{2,1,0:T(8,128)S(1)}, u32[]{:S(2)}, u32[]{:S(2)}) collective-permute-start(f32[2,256,2048]{2,1,0:T(8,128)S(1)} %pad_maximum_fusion), channel_id=1, source_target_pairs={{0,1},{1,0},{2,3},{3,2},{4,5},{5,4},{6,7},{7,6},{8,9},{9,8},{10,11... | collective-permute-start | bytes 12582920 | tf_op jit(solution)/shard_map/ppermute | solution.py:97
  221.5 6.2 %slice-start.3 = ((s8[8388608]{0:T(1024)(128)(4,1)}), s8[4194304]{0:T(1024)(128)(4,1)S(1)}, s32[]{:S(2)}) async-start(s8[8388608]{0:T(1024)(128)(4,1)} %bitcast.129), calls=%async_computation.3 | async-start | bytes 8388608
  227.7 2.5 copy-start.8
  227.7 2.5 copy-start.9
  231.7 1.5 copy-start.7
  231.7 2.5 slice-start
  233.2 2.5 slice-start.1
  233.7 10.1 %slice-start.4 = ((s8[11534336]{0:T(1024)(128)(4,1)}), s8[4194304]{0:T(1024)(128)(4,1)S(1)}, s32[]{:S(2)}) async-start(s8[11534336]{0:T(1024)(128)(4,1)} %bitcast.139), calls=%async_computation.4 | async-start | bytes 8388608
  235.7 8.1 %slice-start.5 = ((s8[11534336]{0:T(1024)(128)(4,1)}), s8[4194304]{0:T(1024)(128)(4,1)S(1)}, s32[]{:S(2)}) async-start(s8[11534336]{0:T(1024)(128)(4,1)} %bitcast.139), calls=%async_computation.5 | async-start | bytes 8388608
  235.7 8.1 %slice-start.6 = ((s8[11534336]{0:T(1024)(128)(4,1)}), s8[3145728]{0:T(1024)(128)(4,1)S(1)}, s32[]{:S(2)}) async-start(s8[11534336]{0:T(1024)(128)(4,1)} %bitcast.139), calls=%async_computation.6 | async-start | bytes 6291456
  238.2 5.6 %copy-start.13 = (f32[2048]{0:T(1024)S(1)}, f32[2048]{0:T(1024)}, u32[]{:S(2)}) copy-start(f32[2048]{0:T(1024)} %convert_element_type.106) | copy-start | bytes 24580
  238.2 1.9 copy-start.5
  242.0 47.9 %collective-permute-start.7 = (f32[256,2048]{1,0:T(8,128)S(1)}, f32[256,2048]{1,0:T(8,128)}, u32[]{:S(2)}, u32[]{:S(2)}) collective-permute-start(f32[256,2048]{1,0:T(8,128)S(1)} %fusion.37), channel_id=1, source_target_pairs={{0,2},{1,3},{2,0},{3,1},{4,6},{5,7},{6,4},{7,5},{8,10},{9,11},{10,... | collective-permute-start | bytes 6291464 | tf_op jit(solution)/shard_map/ppermute | solution.py:98
  248.6 46.4 %copy-start.1 = (bf16[2048,64]{0,1:T(8,128)(2,1)S(1)}, bf16[2048,64]{0,1:T(8,128)(2,1)}, u32[]{:S(2)}) copy-start(bf16[2048,64]{0,1:T(8,128)(2,1)} %param.30) | copy-start | bytes 786436
  (2 other events, 2.2 us)

commit v2 on v1

v2 whole, which is shorter than its diff:
```python
import functools

import jax
import jax.numpy as jnp
from jax import lax
from jax.experimental import pallas as pl
from jax.experimental.pallas import tpu as pltpu
from jax.sharding import PartitionSpec as P

HEAD = 128
EPS = 1e-6
CAP_FACTOR = 2
WIDE = 512
BLK = 256
RING = 8
WSLOTS = 3
MESH = pl.DeviceIdType.MESH
F32, BF16 = jnp.float32, jnp.bfloat16


def _dot(a, b):
    return jnp.dot(a, b, preferred_element_type=F32)


def _rms(x, w):
    xf = x.astype(F32)
    r = lax.rsqrt(jnp.mean(xf * xf, axis=-1, keepdims=True) + EPS)
    return (xf * r * w.astype(F32)).astype(BF16)


def _silu_mul(h1, h3):
    return (h1 * jax.nn.sigmoid(h1) * h3).astype(BF16)


def _gate(u, wr, gi):
    lg = _dot(u, wr)
    hit = gi[..., None] == jnp.arange(wr.shape[1], dtype=gi.dtype)
    return jax.nn.softmax(jnp.sum(jnp.where(hit, lg[:, None, :], 0.0), axis=-1), axis=-1)


def _tables(s):
    half = HEAD // 2
    freq = 10000.0 ** (-jnp.arange(half, dtype=F32) / half)
    ang = jnp.arange(s, dtype=F32)[:, None] * freq[None, :]
    c, sn = jnp.cos(ang), jnp.sin(ang)
    return jnp.concatenate([c, c], axis=-1), jnp.concatenate([-sn, sn], axis=-1)


def _dense_kernel(na, nf, h_ref, la_ref, lf_ref, cos_ref, sin_ref, wq_ref, wk_ref, wv_ref, wo_ref, w1_ref, w3_ref, w2_ref,
                  out_ref, x_ref, acc_ref):
    g = pl.program_id(0)
    t = h_ref.shape[0]

    @pl.when(g == 0)
    def _():
        x_ref[...] = _rms(h_ref[...], la_ref[...])
        acc_ref[...] = jnp.zeros_like(acc_ref)

    @pl.when(g < na)
    def _():
        x = x_ref[...]
        q = _dot(x, wq_ref[...])
        k = _dot(x, wk_ref[...])
        v = _dot(x, wv_ref[...]).astype(BF16)
        c, s = cos_ref[...], sin_ref[...]
        ok = lax.broadcasted_iota(jnp.int32, (t, t), 0) >= lax.broadcasted_iota(jnp.int32, (t, t), 1)
        outs = []
        for i in range(WIDE // HEAD):
            cols = slice(i * HEAD, (i + 1) * HEAD)
            qi, ki = q[:, cols], k[:, cols]
            qi = (qi * c + pltpu.roll(qi, HEAD // 2, 1) * s).astype(BF16)
            ki = (ki * c + pltpu.roll(ki, HEAD // 2, 1) * s).astype(BF16)
            sc = lax.dot_general(qi, ki, (((1,), (1,)), ((), ())), preferred_element_type=F32) * HEAD ** -0.5
            sc = jnp.where(ok, sc, -1e30)
            e = jnp.exp(sc - jnp.max(sc, axis=-1, keepdims=True))
            p = (e / jnp.sum(e, axis=-1, keepdims=True)).astype(BF16)
            outs.append(_dot(p, v[:, cols]).astype(BF16))
        acc_ref[...] += _dot(jnp.concatenate(outs, axis=-1), wo_ref[...])

    @pl.when(g == na - 1)
    def _():
        a = (h_ref[...].astype(F32) + acc_ref[...]).astype(BF16)
        acc_ref[...] = a.astype(F32)
        x_ref[...] = _rms(a, lf_ref[...])

    @pl.when(g >= na)
    def _():
        x = x_ref[...]
        s = _silu_mul(_dot(x, w1_ref[...]), _dot(x, w3_ref[...]))
        acc_ref[...] += _dot(s, w2_ref[...])

    @pl.when(g == na + nf - 1)
    def _():
        for c in range(out_ref.shape[0]):
            out_ref[c] = acc_ref[:, c * BLK:(c + 1) * BLK]


def _dense(h, ln_attn, wq, wk, wv, wo, ln_ffn, ws1, ws3, ws2):
    t, d = h.shape
    na, nf = wq.shape[1] // WIDE, ws1.shape[1] // BLK
    cos, sin = _tables(t)
    full = lambda shape: pl.BlockSpec(shape, lambda g: (0,) * len(shape))
    head = lambda g: jnp.minimum(g, na - 1)
    ffn = lambda g: jnp.maximum(g - na, 0)
    col = lambda w, f: pl.BlockSpec((d, w), lambda g: (0, f(g)))
    row = lambda w, f: pl.BlockSpec((w, d), lambda g: (f(g), 0))
    return pl.pallas_call(
        functools.partial(_dense_kernel, na, nf),
        grid=(na + nf,),
        in_specs=[full((t, d)), full((1, d)), full((1, d)), full((t, HEAD)), full((t, HEAD)),
                  col(WIDE, head), col(WIDE, head), col(WIDE, head), row(WIDE, head),
                  col(BLK, ffn), col(BLK, ffn), row(BLK, ffn)],
        out_specs=full((d // BLK, t, BLK)),
        out_shape=jax.ShapeDtypeStruct((d // BLK, t, BLK), F32),
        scratch_shapes=[pltpu.VMEM((t, d), BF16), pltpu.VMEM((t, d), F32)],
        compiler_params=pltpu.CompilerParams(dimension_semantics=('arbitrary',), vmem_limit_bytes=56 << 20),
        cost_estimate=pl.CostEstimate(flops=2 * t * d * (4 * d + 3 * ws1.shape[1]), transcendentals=0,
                                      bytes_accessed=2 * d * (4 * d + 3 * ws1.shape[1])),
        name='dense',
    )(h, ln_attn[None], ln_ffn[None], cos, sin, wq, wk, wv, wo, ws1, ws3, ws2)


def _expert_kernel(el, cap, top, u0, u1, u2, u3, pt_ref, pk_ref, base_hbm, ue1, ue3, ue2, out_hbm,
                   wbuf, ring, he, ub, xs, ys, cm, sd, rd, sx, rx, base, ob,
                   wsem, rsem, usem, bsem, osem, sd_sem, rd_sem, sx_sem, rx_sem):
    me = lax.axis_index('ep')
    dp = lax.axis_index('dp')
    core = (dp, me + 1 - 2 * lax.rem(me, 2))
    chip = (dp, lax.rem(me + 2, 4))
    fe = ue1.shape[2]
    wa = (fe // 2 + 127) // 128 * 128
    widths = (wa, fe - wa)
    nc = out_hbm.shape[1] // BLK
    first = me * (el * cap)

    def unit(e, h, slot):
        w, lo = widths[h], h * wa
        return [pltpu.make_async_copy(ue.at[e, :, lo:lo + w], wbuf.at[slot, :, k * w:(k + 1) * w], wsem.at[slot, k])
                for k, ue in enumerate((ue1, ue3))]

    def piece(c, e, slot):
        return pltpu.make_async_copy(ue2.at[e, :, pl.ds(pl.multiple_of(c * BLK, BLK), BLK)], ring.at[slot], rsem.at[slot])

    ucopies = [pltpu.make_async_copy(r, ub.at[k], usem.at[k]) for k, r in enumerate((u0, u1, u2, u3))]
    for cp in ucopies:
        cp.start()
    for n in range(WSLOTS):
        for cp in unit(n // 2, n % 2, n):
            cp.start()
    bcopy = pltpu.make_async_copy(base_hbm, base, bsem)
    bcopy.start()

    barrier = pltpu.get_barrier_semaphore()
    for peer in (core, chip):
        pl.semaphore_signal(barrier, inc=1, device_id=peer, device_id_type=MESH)
    pl.semaphore_wait(barrier, 2)

    for k in range(4):
        pos, gate = pk_ref[k, :, :top], pk_ref[k, :, top:2 * top]
        r = (lax.broadcasted_iota(jnp.int32, (pos.shape[0], el * cap), 1) + first).astype(F32)
        c = jnp.zeros(r.shape, F32)
        for j in range(top):
            c += jnp.where(pos[:, j:j + 1] == r, gate[:, j:j + 1], 0.0)
        hi = c.astype(BF16)
        c -= hi.astype(F32)
        mid = c.astype(BF16)
        cm[0, k] = hi
        cm[1, k] = mid
        cm[2, k] = (c - mid.astype(F32)).astype(BF16)

    for cp in ucopies:
        cp.wait()

    def ffn_in(e, _):
        for k in range(4):
            r = lax.broadcasted_iota(jnp.int32, (cap, pt_ref.shape[2]), 0) + (first + e * cap)
            hit = pt_ref[k, 0:1, :] == r
            for j in range(1, top):
                hit = jnp.logical_or(hit, pt_ref[k, j:j + 1, :] == r)
            xs[k * cap:(k + 1) * cap, :] = _dot(hit.astype(F32).astype(BF16), ub[k]).astype(BF16)
        for h in range(2):
            n = 2 * e + h
            slot = lax.rem(n, WSLOTS)
            w = widths[h]
            for cp in unit(e, h, slot):
                cp.wait()
            z = _dot(xs[...], wbuf[slot, :, :2 * w])
            he[e, :, h * wa:h * wa + w] = _silu_mul(z[:, :w], z[:, w:])
            en, hn = e + (h + WSLOTS) // 2, (h + WSLOTS) % 2

            @pl.when(en < el)
            def _():
                for cp in unit(en, hn, slot):
                    cp.start()
        return 0

    lax.fori_loop(0, el - 1, ffn_in, 0)
    for n in range(RING):
        piece(0, n, n).start()
    ffn_in(el - 1, 0)
    bcopy.wait()

    def d2d(c, k):
        return pltpu.make_async_remote_copy(sd.at[lax.rem(c, 2), k], rd.at[c, k], sd_sem.at[lax.rem(c, 2), k], rd_sem.at[c, k],
                                            device_id=core, device_id_type=MESH)

    def x2x(c):
        return pltpu.make_async_remote_copy(sx.at[c], rx.at[c], sx_sem.at[c], rx_sem.at[c],
                                            device_id=chip, device_id_type=MESH)

    def relay(c):
        d2d(c, 1).wait_recv()
        sx[c] += rd[c, 1]
        x2x(c).start()
        d2d(c, 0).wait_recv()
        base[c] += rd[c, 0]

    def chunk(c, _):
        def pair(i, _):
            for h in range(2):
                e = 2 * i + h
                slot = lax.rem(e, RING)
                piece(c, e, slot).wait()
                y = _dot(he[e], ring[slot]).astype(BF16)
                for k in range(4):
                    ys[k, pl.ds(pl.multiple_of(e * cap, cap), cap), :] = y[k * cap:(k + 1) * cap]
                wrap = (e + RING >= el).astype(jnp.int32)

                @pl.when(c + wrap < nc)
                def _():
                    piece(c + wrap, lax.rem(e + RING, el), slot).start()
            return 0

        lax.fori_loop(0, el // 2, pair, 0)

        @pl.when(c >= 2)
        def _():
            for k in range(2):
                d2d(c - 2, k).wait_send()

        def total(k):
            return _dot(cm[0, k], ys[k]) + _dot(cm[1, k], ys[k]) + _dot(cm[2, k], ys[k])

        sd[lax.rem(c, 2), 1] = total(3)
        d2d(c, 1).start()
        sd[lax.rem(c, 2), 0] = total(1)
        d2d(c, 0).start()
        sx[c] = total(2)
        base[c] += total(0)

        @pl.when(c >= 1)
        def _():
            relay(c - 1)
        return 0

    lax.fori_loop(0, nc, chunk, 0)
    relay(nc - 1)
    for c in (nc - 2, nc - 1):
        for k in range(2):
            d2d(c, k).wait_send()

    def put(c):
        return pltpu.make_async_copy(ob.at[c], out_hbm.at[:, pl.ds(pl.multiple_of(c * BLK, BLK), BLK)], osem.at[c])

    def finish(c, _):
        x2x(c).wait_recv()
        ob[c] = (base[c] + rx[c]).astype(BF16)
        put(c).start()
        return 0

    lax.fori_loop(0, nc, finish, 0)

    def drain(c, _):
        x2x(c).wait_send()
        put(c).wait()
        return 0

    lax.fori_loop(0, nc, drain, 0)


def _experts(us, pt, pk, base, ue1, ue3, ue2, top, cap):
    t, d = us[0].shape
    el, _, fe = ue1.shape
    nc = d // BLK
    wa = (fe // 2 + 127) // 128 * 128
    hbm = pl.BlockSpec(memory_space=pl.ANY)
    vmem = pl.BlockSpec(memory_space=pltpu.VMEM)
    dma = pltpu.SemaphoreType.DMA
    return pl.pallas_call(
        functools.partial(_expert_kernel, el, cap, top),
        in_specs=[hbm] * 4 + [vmem] * 2 + [hbm] * 4,
        out_specs=hbm,
        out_shape=jax.ShapeDtypeStruct((t, d), BF16),
        scratch_shapes=[
            pltpu.VMEM((WSLOTS, d, 2 * wa), BF16), pltpu.VMEM((RING, fe, BLK), BF16), pltpu.VMEM((el, 4 * cap, fe), BF16),
            pltpu.VMEM((4, t, d), BF16), pltpu.VMEM((4 * cap, d), BF16), pltpu.VMEM((4, el * cap, BLK), BF16),
            pltpu.VMEM((3, 4, t, el * cap), BF16), pltpu.VMEM((2, 2, t, BLK), F32), pltpu.VMEM((nc, 2, t, BLK), F32),
            pltpu.VMEM((nc, t, BLK), F32), pltpu.VMEM((nc, t, BLK), F32), pltpu.VMEM((nc, t, BLK), F32),
            pltpu.VMEM((nc, t, BLK), BF16),
            dma((WSLOTS, 2)), dma((RING,)), dma((4,)), dma, dma((nc,)), dma((2, 2)), dma((nc, 2)), dma((nc,)), dma((nc,)),
        ],
        compiler_params=pltpu.CompilerParams(collective_id=0, has_side_effects=True, vmem_limit_bytes=67043328),
        cost_estimate=pl.CostEstimate(flops=6 * el * 4 * cap * d * fe, transcendentals=0, bytes_accessed=6 * el * d * fe),
        name='experts',
    )(*us, pt, pk, base, ue1, ue3, ue2)


def solution(mesh):
    rows = P(('dp', 'ep'))
    rep = P()
    core = [(k, k ^ 1) for k in range(4)]
    chip = [(k, k ^ 2) for k in range(4)]

    def local(h0, idx, slot, ln_attn, wq, wk, wv, wo, ln_ffn, ws1, ws3, ws2, ln_moe, wr, ue1, ue3, ue2):
        b, s, d = h0.shape
        top = idx.shape[-1]
        el = ue1.shape[0]
        t = b * s
        cap = CAP_FACTOR * t * top // (el * mesh.shape['ep'])
        h = h0.reshape(t, d)
        u = _rms(h, ln_moe)
        gi = idx.reshape(t, top)
        gate = _gate(u, wr, gi)
        pos = (gi * cap + slot.reshape(t, top)).astype(F32)
        pk = jnp.concatenate([pos, gate], axis=-1)
        ux, kx = lax.ppermute(u, 'ep', chip), lax.ppermute(pk, 'ep', chip)
        uc, kc = lax.ppermute(u, 'ep', core), lax.ppermute(pk, 'ep', core)
        uxc, kxc = lax.ppermute(ux, 'ep', core), lax.ppermute(kx, 'ep', core)
        base = _dense(h, ln_attn, wq, wk, wv, wo, ln_ffn, ws1, ws3, ws2)
        ks = jnp.stack([pk, kc, kx, kxc])
        pt = jnp.transpose(ks[..., :top], (0, 2, 1)).astype(jnp.int32)
        out = _experts((u, uc, ux, uxc), pt, ks, base, ue1, ue3, ue2, top, cap)
        return out.reshape(b, s, d)

    specs = (rows, rows, rows) + (rep,) * 11 + (P('ep'), P('ep'), P('ep'))
    return jax.shard_map(local, mesh=mesh, in_specs=specs, out_specs=rows, check_vma=False)
```

time: 299 us -> 238 us (0.80); the launches traced: 295 us -> 237 us
  Pallas kernels: 0 us -> 200 us
  matrix products: 199 us -> 1.39 us
  local copies, waits for them, and re-layouts: 42 us -> 7.28 us
  other arithmetic: 22.2 us -> 6.03 us
  waiting for transfers between devices: 25.3 us -> 18.4 us
    pallas_call x0 -> x2, Pallas kernels: none -> 200 us  [the longest x1 161 us: _experts(): pl.pallas_call(functools.partial(_expert_kernel, el, cap, top), in_specs=...]
    dot_general x16 -> x1, matrix products: 199 us -> 1.39 us  [_dot(): return jnp.dot(a, b, preferred_element_type=F32)]
    ppermute x2 -> x0, waiting for transfers between devices: 25.3 us -> none  [the longest x1 25.3 us: local(): far = lax.ppermute(m[2] + got[1], 'ep', chip)]
    dot_general x2 -> x0, local copies, waits for them, and re-layouts: 25 us -> none  [_mm(): return jnp.einsum(form, a, b, preferred_element_type=jnp.float32)]
    ppermute x2, waiting for transfers between devices: 0.01 us -> 18.4 us  [local(): ux, kx = (lax.ppermute(u, 'ep', chip), lax.ppermute(pk, 'ep', chip))]
    convert_element_type x1, local copies, waits for them, and re-layouts: 6.45 us -> 0.79 us  [local(): pt = jnp.transpose(ks[..., :top], (0, 2, 1)).astype(jnp.int32)]
    convert_element_type x6 -> x4, other arithmetic: 7.93 us -> 2.98 us  [the longest x2 2.22 us: _rms(): return (xf * r * w.astype(F32)).astype(BF16)]
    reduce_or x1 -> x0, other arithmetic: 3.12 us -> none  [local(): disp = jnp.any(hit, axis=-2).astype(jnp.bfloat16)]
  transfers between devices with their start and end apart: 8 -> 6, of which waited for: 1 -> 1; matrix products, arithmetic and copies ran while one was open for 26% -> 3% of each run, Pallas kernels for 0% -> 16%
where the time goes in v2:
time: 238 us; the launch traced here: 237 us
  Pallas kernels  200 us (84%)
  waiting for transfers between devices  18.4 us (8%)
  local copies, waits for them, and re-layouts  7.28 us (3%)
  other arithmetic  6.03 us (3%)
  starting transfers between devices  4.35 us (2%)
    pallas_call x1, Pallas kernels, _experts(): pl.pallas_call(functools.partial(_expert_kernel, el, cap, top), in_specs=...  161 us
    pallas_call x1, Pallas kernels, _dense(): pl.pallas_call(functools.partial(_dense_kernel, na, nf), grid=(na + nf,),...  38.6 us
    ppermute x2, waiting for transfers between devices, local(): ux, kx = (lax.ppermute(u, 'ep', chip), lax.ppermute(pk, 'ep', chip))  18.4 us
  transfers between devices with their start and end apart: 6, of which 1 were waited for; matrix products, arithmetic and copies ran while one was open for 3% of the time, Pallas kernels for 16%

profile of v2, /device:TPU:0, one launch (start us, length us, event | category | flops | bytes accessed | tf_op | source)
XLA Modules:
  0.0 237.4 jit_solution(15566309776350171374)
XLA Ops:
  0.0 1.5 fusion
  1.5 0.7 convert_element_type.18
  2.2 1.5 fusion.2.u0
  3.8 0.0 copy-start
  3.8 3.3 %collective-permute-start.1 = (bf16[256,2048]{1,0:T(8,128)(2,1)S(1)}, bf16[256,2048]{1,0:T(8,128)(2,1)S(1)}, u32[]{:S(2)}, u32[]{:S(2)}) collective-permute-start(bf16[256,2048]{1,0:T(8,128)(2,1)S(1)} %fusion.2.u0), channel_id=1, source_target_pairs={{0,2},{1,3},{2,0},{3,1},{4,6},{5,7},{6,4},{7,5},{8,10},{9,11},{10,... | collective-permute-start | bytes 3145736 | tf_op jit(solution)/shard_map/ppermute | solution.py:326
  7.0 0.7 copy.40
  7.7 1.4 fusion.10
  9.1 0.1 select_reduce_fusion
  9.2 0.7 fusion.7
  10.0 0.1 copy.30
  10.1 0.1 collective-permute-start.4
  10.2 0.0 collective-permute-start.3
  10.2 0.5 collective-permute-start
  10.7 0.5 fusion.6
  11.2 0.8 pad_maximum_fusion.1
  12.1 1.3 broadcast_in_dim.28.la_ref
  13.3 1.3 broadcast_in_dim.29.lf_ref
  14.6 18.4 %collective-permute-done.4 = f32[256,12]{1,0:T(8,128)S(1)} collective-permute-done((f32[256,12]{1,0:T(8,128)S(1)}, f32[256,12]{1,0:T(8,128)S(1)}, u32[]{:S(2)}, u32[]{:S(2)}) %collective-permute-start.4) | collective-permute-done | bytes 12320 | tf_op jit(solution)/shard_map/ppermute | solution.py:326
  33.0 0.0 collective-permute-start.5
  33.0 0.0 collective-permute-done.1.u2
  33.0 0.5 collective-permute-start.2
  33.5 38.6 %dense.1.base_hbm = f32[8,256,256]{2,1,0:T(8,128)} custom-call(bf16[256,2048]{1,0:T(8,128)(2,1)} %bitcast.21, bf16[1,2048]{1,0:T(2,128)(2,1)} %broadcast_in_dim.28.la_ref, bf16[1,2048]{1,0:T(2,128)(2,1)} %broadcast_in_dim.29.lf_ref, f32[256,128]{1,0:T(8,128)} %get-tuple-element.8.cos_ref, f32[256,128]{1,0:T(8,128)} %get-tuple-element.9.sin_ref, ...), custom_call_target="tpu_custom_call" | custom-call | flops 17448304640 | bytes 68157440 | tf_op jit(solution)/shard_map/dense/pallas_call | solution.py:107
  72.1 0.0 copy-done
  72.1 0.0 copy-done.2
  72.2 0.0 collective-permute-done.3
  72.2 0.0 collective-permute-done.5
  72.2 0.8 copy-done.1
  73.1 0.8 copy.33.pt_ref
  73.9 0.0 collective-permute-done.u1
  73.9 0.0 collective-permute-done.2.u3
  73.9 161.2 %experts.1 = bf16[256,2048]{1,0:T(8,128)(2,1)} custom-call(bf16[256,2048]{1,0:T(8,128)(2,1)} %copy-done, bf16[256,2048]{1,0:T(8,128)(2,1)} %collective-permute-done.u1, bf16[256,2048]{1,0:T(8,128)(2,1)} %copy-done.2, bf16[256,2048]{1,0:T(8,128)(2,1)} %collective-permute-done.2.u3, s32[4,6,256]{2,1,0:T(8,128)} %copy.33.pt_ref, f32[4,256,12]{2,1,0:T(8,128)} %copy-done.1, ...), custom_call_target="tpu_custom_call" | custom-call | flops 53150220288 | bytes 276824064 | tf_op jit(solution)/shard_map/experts/pallas_call | solution.py:289
  235.1 2.3 copy.42
  (10 shorter events, 0.2 us)
Async XLA Ops:
  3.8 68.4 %copy-start = (bf16[256,2048]{1,0:T(8,128)(2,1)}, bf16[256,2048]{1,0:T(8,128)(2,1)S(1)}, u32[]{:S(2)}) copy-start(bf16[256,2048]{1,0:T(8,128)(2,1)S(1)} %fusion.2.u0) | copy-start | bytes 3145732
  3.8 29.2 %collective-permute-start.1 = (bf16[256,2048]{1,0:T(8,128)(2,1)S(1)}, bf16[256,2048]{1,0:T(8,128)(2,1)S(1)}, u32[]{:S(2)}, u32[]{:S(2)}) collective-permute-start(bf16[256,2048]{1,0:T(8,128)(2,1)S(1)} %fusion.2.u0), channel_id=1, source_target_pairs={{0,2},{1,3},{2,0},{3,1},{4,6},{5,7},{6,4},{7,5},{8,10},{9,11},{10,... | collective-permute-start | bytes 3145736 | tf_op jit(solution)/shard_map/ppermute | solution.py:326
  10.1 22.9 %collective-permute-start.4 = (f32[256,12]{1,0:T(8,128)S(1)}, f32[256,12]{1,0:T(8,128)S(1)}, u32[]{:S(2)}, u32[]{:S(2)}) collective-permute-start(f32[256,12]{1,0:T(8,128)S(1)} %copy.30), channel_id=1, source_target_pairs={{0,2},{1,3},{2,0},{3,1},{4,6},{5,7},{6,4},{7,5},{8,10},{9,11},{10,... | collective-permute-start | bytes 36872 | tf_op jit(solution)/shard_map/ppermute | solution.py:326
  10.2 62.0 %collective-permute-start.3 = (f32[256,12]{1,0:T(8,128)S(1)}, f32[256,12]{1,0:T(8,128)S(1)}, u32[]{:S(2)}, u32[]{:S(2)}) collective-permute-start(f32[256,12]{1,0:T(8,128)S(1)} %copy.30), channel_id=1, source_target_pairs={{0,1},{1,0},{2,3},{3,2},{4,5},{5,4},{6,7},{7,6},{8,9},{9,8},{10,11... | collective-permute-start | bytes 36872 | tf_op jit(solution)/shard_map/ppermute | solution.py:327
  10.2 63.7 %collective-permute-start = (bf16[256,2048]{1,0:T(8,128)(2,1)S(1)}, bf16[256,2048]{1,0:T(8,128)(2,1)}, u32[]{:S(2)}, u32[]{:S(2)}) collective-permute-start(bf16[256,2048]{1,0:T(8,128)(2,1)S(1)} %fusion.2.u0), channel_id=1, source_target_pairs={{0,1},{1,0},{2,3},{3,2},{4,5},{5,4},{6,7},{7,6},{8,9},{9,8},{10,11... | collective-permute-start | bytes 3145736 | tf_op jit(solution)/shard_map/ppermute | solution.py:327
  33.0 39.2 %collective-permute-start.5 = (f32[256,12]{1,0:T(8,128)S(1)}, f32[256,12]{1,0:T(8,128)S(1)}, u32[]{:S(2)}, u32[]{:S(2)}) collective-permute-start(f32[256,12]{1,0:T(8,128)S(1)} %collective-permute-done.4), channel_id=1, source_target_pairs={{0,1},{1,0},{2,3},{3,2},{4,5},{5,4},{6,7},{7,6},{8,9},{9,8},{10,11... | collective-permute-start | bytes 36872 | tf_op jit(solution)/shard_map/ppermute | solution.py:328
  33.0 39.1 %copy-start.2 = (bf16[256,2048]{1,0:T(8,128)(2,1)}, bf16[256,2048]{1,0:T(8,128)(2,1)S(1)}, u32[]{:S(2)}) copy-start(bf16[256,2048]{1,0:T(8,128)(2,1)S(1)} %collective-permute-done.1.u2) | copy-start | bytes 3145732
  33.0 40.9 %collective-permute-start.2 = (bf16[256,2048]{1,0:T(8,128)(2,1)S(1)}, bf16[256,2048]{1,0:T(8,128)(2,1)}, u32[]{:S(2)}, u32[]{:S(2)}) collective-permute-start(bf16[256,2048]{1,0:T(8,128)(2,1)S(1)} %collective-permute-done.1.u2), channel_id=1, source_target_pairs={{0,1},{1,0},{2,3},{3,2},{4,5},{5,4},{6,7},{7,6},{8,9},{9,8},{10,11... | collective-permute-start | bytes 3145736 | tf_op jit(solution)/shard_map/ppermute | solution.py:328
  72.2 0.8 copy-start.1

commit v3 on v0

v3 whole, which is shorter than its diff:
```python
import functools

import jax
import jax.numpy as jnp
import numpy as np
from jax import lax
from jax.experimental import pallas as pl
from jax.experimental.pallas import tpu as pltpu
from jax.sharding import PartitionSpec as P

HEAD = 128
EPS = 1e-6
CAP_FACTOR = 2
BLK = 256
RING = 8
SLOTS = 3
GROUP = 4
PIECES = 4
MESH = pl.DeviceIdType.MESH
F32, BF16 = jnp.float32, jnp.bfloat16


def _dot(a, b):
    return jnp.dot(a, b, preferred_element_type=F32)


def _rms(x, w):
    xf = x.astype(F32)
    r = lax.rsqrt(jnp.mean(xf * xf, axis=-1, keepdims=True) + EPS)
    return (xf * r * w).astype(BF16)


def _silu_mul(h1, h3):
    return (h1 * jax.nn.sigmoid(h1) * h3).astype(BF16)


def _tables(s):
    half = HEAD // 2
    freq = np.float32(10000.0) ** (-np.arange(half, dtype=np.float32) / np.float32(half))
    ang = np.arange(s, dtype=np.float32)[:, None] * freq[None, :]
    c, sn = np.cos(ang), np.sin(ang)
    return np.stack([np.concatenate([c, c], axis=-1), np.concatenate([-sn, sn], axis=-1)]).astype(np.float32)


def _layer(el, cap, top, h_ref, pt_ref, ln_ref, tab_ref, wr_ref, wq, wk, wv, wo, ws1, ws3, ws2, ue1, ue3, ue2, out_hbm,
           wbuf, ring, he, ub, xa, sb, x4, ys, cm, pts, sd, rd, sx, rx, base, ob,
           wsem, rsem, osem, hs_sem, hr_sem, ps_sem, pr_sem, sd_sem, rd_sem, sx_sem, rx_sem):
    me = lax.axis_index('ep')
    dp = lax.axis_index('dp')
    core = (dp, me + 1 - 2 * lax.rem(me, 2))
    chip = (dp, lax.rem(me + 2, 4))
    t, d = h_ref.shape
    fe, fs = ue1.shape[2], ws1.shape[1]
    wide = wbuf.shape[2]
    wa = wide // 2
    widths = (wa, fe - wa)
    nc = d // BLK
    hw = wide // 3
    na = d // hw
    first = me * (el * cap)

    def load(src, dst, sem):
        return pltpu.make_async_copy(src, dst, sem)

    def send(src, dst, s, r, peer):
        return pltpu.make_async_remote_copy(src, dst, s, r, device_id=peer, device_id_type=MESH)

    def qkv(i, slot):
        cols = pl.ds(pl.multiple_of(i * hw, hw), hw)
        return [load(w.at[:, cols], wbuf.at[slot, :, k * hw:(k + 1) * hw], wsem.at[slot, k])
                for k, w in enumerate((wq, wk, wv))]

    wo_a = [load(wo.at[:, :wide], wbuf.at[na % SLOTS], wsem.at[na % SLOTS, 0])]
    wo_b = [load(wo.at[:, wide:], wbuf.at[(na + 1) % SLOTS, :, :d - wide], wsem.at[(na + 1) % SLOTS, 0])]

    def unit(e, h, slot):
        w, lo = widths[h], h * wa
        return [load(ue.at[e, :, lo:lo + w], wbuf.at[slot, :, k * w:(k + 1) * w], wsem.at[slot, k])
                for k, ue in enumerate((ue1, ue3))]

    def piece(c, e, slot):
        return load(ue2.at[e, :, pl.ds(pl.multiple_of(c * BLK, BLK), BLK)], ring.at[slot], rsem.at[slot])

    def shared_in(k):
        lo, w = k * wa, min(wa, fs - k * wa)
        return [load(ws.at[:, lo:lo + w], wbuf.at[k % SLOTS, :, i * w:(i + 1) * w], wsem.at[k % SLOTS, i])
                for i, ws in enumerate((ws1, ws3))]

    ns = -(-fs // wa)
    slot_a, slot_b = ns % SLOTS, (ns + 1) % SLOTS
    rest, tail = fs - d, d - wide
    half = wide - tail
    shared_a = [load(ws2.at[:d, :wide], wbuf.at[slot_a], wsem.at[slot_a, 0])]
    shared_b = [load(ws2.at[:d, wide:], wbuf.at[slot_b, :, :tail], wsem.at[slot_b, 0]),
                load(ws2.at[d:, :half], wbuf.at[slot_b, :rest, tail:], wsem.at[slot_b, 1]),
                load(ws2.at[d:, half:], wbuf.at[slot_b, rest:2 * rest, tail:], wsem.at[slot_b, 2])]

    def start(copies):
        for cp in copies:
            cp.start()

    def wait(copies):
        for cp in copies:
            cp.wait()

    for n in range(SLOTS):
        start(qkv(n, n))

    barrier = pltpu.get_barrier_semaphore()
    for peer in (core, chip):
        pl.semaphore_signal(barrier, inc=1, device_id=peer, device_id_type=MESH)
    pl.semaphore_wait(barrier, 2)

    rows = t // PIECES
    part = [pl.ds(q * rows, rows) for q in range(PIECES)]
    far = [send(h_ref.at[part[q]], ub.at[2, part[q]], hs_sem.at[q], hr_sem.at[q], chip) for q in range(PIECES)]
    near = send(h_ref, ub.at[1], hs_sem.at[PIECES], hr_sem.at[PIECES], core)
    onward = [send(ub.at[2, part[q]], ub.at[3, part[q]], hs_sem.at[PIECES + 1 + q], hr_sem.at[PIECES + 1 + q], core)
              for q in range(PIECES)]
    pfar = send(pt_ref, pts.at[2], ps_sem.at[0], pr_sem.at[0], chip)
    pnear = send(pt_ref, pts.at[1], ps_sem.at[1], pr_sem.at[1], core)
    ponward = send(pts.at[2], pts.at[3], ps_sem.at[2], pr_sem.at[2], core)
    pfar.start()
    start(far)
    pnear.start()
    near.start()

    xa[...] = _rms(h_ref[...], ln_ref[0:1, :])
    ub[0] = _rms(h_ref[...], ln_ref[2:3, :])
    pts[0] = pt_ref[...]

    def heads(i, _):
        slot = lax.rem(i, SLOTS)
        wait(qkv(i, slot))
        z = _dot(xa[...], wbuf[slot])

        @pl.when(i + SLOTS < na)
        def _():
            start(qkv(i + SLOTS, slot))

        for k, nxt in enumerate((wo_a, wo_b, unit(0, 0, (na + 2) % SLOTS))):
            @pl.when(i + SLOTS == na + k)
            def _():
                start(nxt)

        c, s = tab_ref[0], tab_ref[1]
        ok = lax.broadcasted_iota(jnp.int32, (t, t), 0) >= lax.broadcasted_iota(jnp.int32, (t, t), 1)
        outs = []
        for j in range(hw // HEAD):
            qj, kj, vj = (z[:, m * hw + j * HEAD:m * hw + (j + 1) * HEAD] for m in range(3))
            qj = (qj * c + pltpu.roll(qj, HEAD // 2, 1) * s).astype(BF16)
            kj = (kj * c + pltpu.roll(kj, HEAD // 2, 1) * s).astype(BF16)
            sc = lax.dot_general(qj, kj, (((1,), (1,)), ((), ())), preferred_element_type=F32) * HEAD ** -0.5
            sc = jnp.where(ok, sc, -1e30)
            e = jnp.exp(sc - jnp.max(sc, axis=-1, keepdims=True))
            p = (e / jnp.sum(e, axis=-1, keepdims=True)).astype(BF16)
            outs.append(_dot(p, vj.astype(BF16)).astype(BF16))
        sb[:, pl.ds(pl.multiple_of(i * hw, hw), hw)] = jnp.concatenate(outs, axis=-1)
        return 0

    lax.fori_loop(0, na, heads, 0)

    def pass_on(q):
        far[q].wait_recv()
        onward[q].start()

    pfar.wait_recv()
    ponward.start()
    pass_on(0)
    pass_on(1)

    def residual(z, lo):
        a = (h_ref[:, lo:lo + z.shape[1]].astype(F32) + z).astype(BF16)
        xa[:, lo:lo + z.shape[1]] = a
        for c in range(z.shape[1] // BLK):
            base[lo // BLK + c] = a[:, c * BLK:(c + 1) * BLK].astype(F32)

    wait(wo_a)
    residual(_dot(sb[:, :d], wbuf[na % SLOTS]), 0)
    start(unit(0, 1, na % SLOTS))
    wait(wo_b)
    residual(_dot(sb[:, :d], wbuf[(na + 1) % SLOTS, :, :d - wide]), wide)
    start(unit(1, 0, (na + 1) % SLOTS))
    xa[...] = _rms(xa[...], ln_ref[1:2, :])
    pass_on(2)

    def weigh(k):
        pos = jnp.concatenate([pts[k].astype(F32), jnp.zeros((HEAD - pts.shape[1], t), F32)], axis=0).T
        lg = _dot(ub[k], wr_ref[...])
        lo = lax.broadcasted_iota(jnp.int32, lg.shape, 1).astype(F32) * cap
        picks = []
        for j in range(top):
            off = pos[:, j:j + 1] - lo
            hit = jnp.logical_and(off >= 0, off < cap)
            picks.append(jnp.sum(jnp.where(hit, lg, 0.0), axis=-1, keepdims=True))
        big = functools.reduce(jnp.maximum, picks)
        ex = [jnp.exp(p - big) for p in picks]
        tot = functools.reduce(jnp.add, ex)
        r = (lax.broadcasted_iota(jnp.int32, (t, el * cap), 1) + first).astype(F32)
        c = jnp.zeros(r.shape, F32)
        for j in range(top):
            c += jnp.where(pos[:, j:j + 1] == r, ex[j] / tot, 0.0)
        hi = c.astype(BF16)
        c -= hi.astype(F32)
        mid = c.astype(BF16)
        cm[k, :t] = hi
        cm[k, t:2 * t] = mid
        cm[k, 2 * t:] = (c - mid.astype(F32)).astype(BF16)

    near.wait_recv()
    pnear.wait_recv()
    ub[1] = _rms(ub[1], ln_ref[2:3, :])

    def weigh_body(k, _):
        weigh(k)
        return 0

    lax.fori_loop(0, 2, weigh_body, 0)
    pass_on(3)
    for cp in onward:
        cp.wait_send()
    ub[2] = _rms(ub[2], ln_ref[2:3, :])
    for cp in onward:
        cp.wait_recv()
    ub[3] = _rms(ub[3], ln_ref[2:3, :])
    ponward.wait()
    pfar.wait_send()
    pnear.wait_send()
    near.wait_send()
    for cp in far:
        cp.wait_send()

    off = (na + 2) % SLOTS

    def group(g, last):
        for k in range(4):
            r = lax.broadcasted_iota(jnp.int32, (GROUP * cap, t), 0) + (first + g * (GROUP * cap))
            hit = pts[k, 0:1, :] == r
            for j in range(1, top):
                hit = jnp.logical_or(hit, pts[k, j:j + 1, :] == r)
            x = _dot(hit.astype(F32).astype(BF16), ub[k]).astype(BF16)
            for j in range(GROUP):
                x4[j, k * cap:(k + 1) * cap, :] = x[j * cap:(j + 1) * cap]

        @pl.when(g < 2)
        def _():
            weigh(g + 2)

        def ffn_in(j, _):
            e = g * GROUP + j
            for h in range(2):
                slot = lax.rem(2 * e + h + off, SLOTS)
                w = widths[h]
                wait(unit(e, h, slot))
                z = _dot(x4[j], wbuf[slot, :, :2 * w])
                he[e, :, h * wa:h * wa + w] = _silu_mul(z[:, :w], z[:, w:])
                en, hn = e + (h + SLOTS) // 2, (h + SLOTS) % 2

                @pl.when(en < el)
                def _():
                    start(unit(en, hn, slot))

                if h == 0:
                    @pl.when(e == el - 1)
                    def _():
                        for n in range(RING):
                            piece(0, n, n).start()
            return 0

        lax.fori_loop(0, GROUP, ffn_in, 0)
        return last

    lax.fori_loop(0, el // GROUP, group, 0)

    def d2d(c, k):
        p = lax.rem(c, 2)
        return send(sd.at[p, k], rd.at[p, k], sd_sem.at[p, k], rd_sem.at[p, k], core)

    def x2x(c):
        return send(sx.at[c], rx.at[c], sx_sem.at[c], rx_sem.at[c], chip)

    def chunk(c, _):
        def quad(i, _):
            s0 = GROUP * lax.rem(i, RING // GROUP)
            for k in range(GROUP):
                piece(c, GROUP * i + k, s0 + k).wait()
            for k in range(GROUP):
                e = GROUP * i + k
                y = _dot(he[e], ring[s0 + k]).astype(BF16)
                for b in range(4):
                    ys[b, pl.ds(pl.multiple_of(e * cap, cap), cap), :] = y[b * cap:(b + 1) * cap]
            wrap = (GROUP * i + RING >= el).astype(jnp.int32)

            @pl.when(c + wrap < nc)
            def _():
                for k in range(GROUP):
                    piece(c + wrap, lax.rem(GROUP * i + RING, el) + k, s0 + k).start()
            return 0

        lax.fori_loop(0, el // GROUP, quad, 0)

        for k in range(SLOTS):
            @pl.when(c == k + 1)
            def _():
                start(shared_in(k))

        @pl.when(c >= 2)
        def _():
            for k in range(2):
                d2d(c - 2, k).wait_send()

        def total(k):
            z = _dot(cm[k], ys[k])
            return z[:t] + z[t:2 * t] + z[2 * t:]

        sd[lax.rem(c, 2), 1] = total(3)
        d2d(c, 1).start()
        sx[c] = total(2)
        sd[lax.rem(c, 2), 0] = total(1)
        d2d(c, 0).start()
        base[c] += total(0)
        d2d(c, 1).wait_recv()
        sx[c] += rd[lax.rem(c, 2), 1]
        x2x(c).start()
        d2d(c, 0).wait_recv()
        base[c] += rd[lax.rem(c, 2), 0]
        return 0

    lax.fori_loop(0, nc, chunk, 0)
    for c in (nc - 2, nc - 1):
        for k in range(2):
            d2d(c, k).wait_send()

    for k in range(ns):
        wait(shared_in(k))
        w = min(wa, fs - k * wa)
        z = _dot(xa[...], wbuf[k % SLOTS, :, :2 * w])
        sb[:, k * wa:k * wa + w] = _silu_mul(z[:, :w], z[:, w:])
        if k + SLOTS < ns:
            start(shared_in(k + SLOTS))
        elif k + SLOTS == ns:
            start(shared_a)
        elif k + SLOTS == ns + 1:
            start(shared_b)

    def add(z, lo):
        for c in range(z.shape[1] // BLK):
            base[lo // BLK + c] += z[:, c * BLK:(c + 1) * BLK]

    wait(shared_a)
    add(_dot(sb[:, :d], wbuf[slot_a]), 0)
    wait(shared_b)
    add(_dot(sb[:, :d], wbuf[slot_b, :, :tail]), wide)
    add(_dot(sb[:, d:], wbuf[slot_b, :rest, tail:]), 0)
    add(_dot(sb[:, d:], wbuf[slot_b, rest:2 * rest, tail:]), half)

    def put(c):
        return load(ob.at[c], out_hbm.at[:, pl.ds(pl.multiple_of(c * BLK, BLK), BLK)], osem.at[c])

    def finish(c, _):
        x2x(c).wait_recv()
        ob[c] = (base[c] + rx[c]).astype(BF16)
        put(c).start()
        return 0

    lax.fori_loop(0, nc, finish, 0)

    def drain(c, _):
        x2x(c).wait_send()
        put(c).wait()
        return 0

    lax.fori_loop(0, nc, drain, 0)


def solution(mesh):
    rows = P(('dp', 'ep'))
    rep = P()

    def local(h0, idx, slot, ln_attn, wq, wk, wv, wo, ln_ffn, ws1, ws3, ws2, ln_moe, wr, ue1, ue3, ue2):
        b, s, d = h0.shape
        top = idx.shape[-1]
        el, _, fe = ue1.shape
        fs = ws1.shape[1]
        t = b * s
        cap = CAP_FACTOR * t * top // (el * mesh.shape['ep'])
        nc = d // BLK
        wide = 2 * ((fe // 2 + HEAD - 1) // HEAD * HEAD)
        pos = (idx * cap + slot).reshape(t, top)
        pt = jnp.pad(pos.T, ((0, 8 - top), (0, 0)), constant_values=-1)
        lns = jnp.stack([ln_attn, ln_ffn, ln_moe]).astype(F32)
        hbm = pl.BlockSpec(memory_space=pl.ANY)
        vmem = pl.BlockSpec(memory_space=pltpu.VMEM)
        dma = pltpu.SemaphoreType.DMA
        out = pl.pallas_call(
            functools.partial(_layer, el, cap, top),
            in_specs=[vmem] * 5 + [hbm] * 10,
            out_specs=hbm,
            out_shape=jax.ShapeDtypeStruct((t, d), BF16),
            scratch_shapes=[
                pltpu.VMEM((SLOTS, d, wide), BF16), pltpu.VMEM((RING, fe, BLK), BF16), pltpu.VMEM((el, 4 * cap, fe), BF16),
                pltpu.VMEM((4, t, d), BF16), pltpu.VMEM((t, d), BF16), pltpu.VMEM((t, fs), BF16),
                pltpu.VMEM((GROUP, 4 * cap, d), BF16), pltpu.VMEM((4, el * cap, BLK), BF16),
                pltpu.VMEM((4, 3 * t, el * cap), BF16), pltpu.VMEM((4, 8, t), jnp.int32),
                pltpu.VMEM((2, 2, t, BLK), F32), pltpu.VMEM((2, 2, t, BLK), F32),
                pltpu.VMEM((nc, t, BLK), F32), pltpu.VMEM((nc, t, BLK), F32), pltpu.VMEM((nc, t, BLK), F32),
                pltpu.VMEM((nc, t, BLK), BF16),
                dma((SLOTS, 3)), dma((RING,)), dma((nc,)), dma((2 * PIECES + 1,)), dma((2 * PIECES + 1,)), dma((3,)), dma((3,)),
                dma((2, 2)), dma((2, 2)), dma((nc,)), dma((nc,)),
            ],
            compiler_params=pltpu.CompilerParams(collective_id=0, has_side_effects=True, vmem_limit_bytes=67043328),
            name='layer',
        )(h0.reshape(t, d), pt, lns, jnp.asarray(_tables(s)), wr, wq, wk, wv, wo, ws1, ws3, ws2, ue1, ue3, ue2)
        return out.reshape(b, s, d)

    specs = (rows, rows, rows) + (rep,) * 11 + (P('ep'), P('ep'), P('ep'))
    return jax.shard_map(local, mesh=mesh, in_specs=specs, out_specs=rows, check_vma=False)
```

time: 471 us -> 166 us (0.35); the launches traced: 464 us -> 165 us
  matrix products: 199 us -> 0 us
  waiting for transfers between devices: 198 us -> 0 us
  Pallas kernels: 0 us -> 157 us
  local copies, waits for them, and re-layouts: 38.9 us -> 6.93 us
  starting transfers between devices: 13.3 us -> 0 us
  other arithmetic: 14.1 us -> 1.34 us
    dot_general x16 -> x0, matrix products: 199 us -> none  [_mm(): return jnp.einsum(form, a, b, preferred_element_type=jnp.float32)]
    all_to_all x2 -> x0, waiting for transfers between devices: 198 us -> none  [the longest x1 138 us: local(): recv = lax.all_to_all(send, 'ep', 0, 0, tiled=True)]
    pallas_call x0 -> x1, Pallas kernels: none -> 157 us  [local(): pl.pallas_call(functools.partial(_layer, el, cap, top), in_specs=[vmem] *...]
    dot_general x2 -> x0, local copies, waits for them, and re-layouts: 24.7 us -> none  [_mm(): return jnp.einsum(form, a, b, preferred_element_type=jnp.float32)]
    all_to_all x2 -> x0, starting transfers between devices: 13.3 us -> none  [the longest x1 6.66 us: local(): back = lax.all_to_all(y, 'ep', 0, 0, tiled=True).reshape(ne * cap, d)]
    convert_element_type x1 -> x0, local copies, waits for them, and re-layouts: 10.7 us -> none  [_experts(): return _mm('egcf,efd->gecd', he, ue2).astype(jnp.bfloat16)]
    reduce_sum x4 -> x0, other arithmetic: 5.78 us -> none  [the longest x1 4.15 us: _route(): comb = jnp.sum(jnp.where(hit, gate[..., None], 0.0), axis=-2)]
  transfers between devices with their start and end apart: 2 -> 0, of which waited for: 2 -> 0; matrix products, arithmetic and copies ran while one was open for 16% -> 0% of each run, Pallas kernels for 0% -> 0%
where the time goes in v3:
time: 166 us; the launch traced here: 165 us
  Pallas kernels  157 us (95%)
  local copies, waits for them, and re-layouts  6.93 us (4%)
    pallas_call x1, Pallas kernels, local(): pl.pallas_call(functools.partial(_layer, el, cap, top), in_specs=[vmem] *...  157 us
    unnamed x2, local copies, waits for them, and re-layouts  4.26 us

profile of v3, /device:TPU:0, one launch (start us, length us, event | category | flops | bytes accessed | tf_op | source)
XLA Modules:
  0.0 165.3 jit_solution(12445016084311251891)
XLA Ops:
  0.0 0.7 fusion
  0.7 0.6 pad.4.pt_ref
  1.3 0.7 stack.12
  2.0 0.7 stack.13
  2.7 0.7 stack.14
  3.4 0.6 maximum_convert_fusion.ln_ref
  4.0 2.0 %copy.21.wr_ref = bf16[2048,64]{1,0:T(8,128)(2,1)} copy(bf16[2048,64]{0,1:T(8,128)(2,1)} %param.31) | data formatting | bytes 524288 | tf_op args[13]
  6.0 157.0 %layer.1 = bf16[256,2048]{1,0:T(8,128)(2,1)} custom-call(bf16[256,2048]{1,0:T(8,128)(2,1)} %bitcast.7, s32[8,256]{1,0:T(8,128)} %pad.4.pt_ref, f32[3,2048]{1,0:T(4,128)} %maximum_convert_fusion.ln_ref, f32[2,256,128]{2,1,0:T(8,128)} %constant.6.clone.tab_ref, bf16[2048,64]{1,0:T(8,128)(2,1)} %copy.21.wr_ref, bf16[2048,2048]{1,0:T(8,128)(2,1)} %wq.1, ...), custom_call_target="tpu_custom_call" | custom-call | tf_op jit(solution)/shard_map/layer/pallas_call | solution.py:395
  163.0 2.3 %copy.29 = bf16[1,256,2048]{2,1,0:T(8,128)(2,1)} copy(bf16[1,256,2048]{2,1,0:T(8,128)(2,1)} %bitcast.6) | data formatting | bytes 2097152

commit v4 on v3

--- a/solution.py
+++ b/solution.py
@@ -42,9 +42,9 @@
     return np.stack([np.concatenate([c, c], axis=-1), np.concatenate([-sn, sn], axis=-1)]).astype(np.float32)
 
 
-def _layer(el, cap, top, h_ref, pt_ref, ln_ref, tab_ref, wr_ref, wq, wk, wv, wo, ws1, ws3, ws2, ue1, ue3, ue2, out_hbm,
-           wbuf, ring, he, ub, xa, sb, x4, ys, cm, pts, sd, rd, sx, rx, base, ob,
-           wsem, rsem, osem, hs_sem, hr_sem, ps_sem, pr_sem, sd_sem, rd_sem, sx_sem, rx_sem):
+def _layer(el, cap, top, idx_ref, slot_ref, la_ref, lf_ref, lm_ref, h_hbm, tab_hbm, wr_hbm, wq, wk, wv, wo, ws1, ws3, ws2, ue1, ue3, ue2, out_hbm,
+           h_ref, tab_ref, wr_ref, wbuf, ring, he, ub, xa, sb, x4, ys, cm, pts, sd, rd, sx, rx, base, ob,
+           isem, wsem, rsem, osem, hs_sem, hr_sem, ps_sem, pr_sem, sd_sem, rd_sem, sx_sem, rx_sem):
     me = lax.axis_index('ep')
     dp = lax.axis_index('dp')
     core = (dp, me + 1 - 2 * lax.rem(me, 2))
@@ -83,11 +83,13 @@
 
     def shared_in(k):
         lo, w = k * wa, min(wa, fs - k * wa)
-        return [load(ws.at[:, lo:lo + w], wbuf.at[k % SLOTS, :, i * w:(i + 1) * w], wsem.at[k % SLOTS, i])
+        n = (n0 + k) % SLOTS
+        return [load(ws.at[:, lo:lo + w], wbuf.at[n, :, i * w:(i + 1) * w], wsem.at[n, i])
                 for i, ws in enumerate((ws1, ws3))]
 
     ns = -(-fs // wa)
-    slot_a, slot_b = ns % SLOTS, (ns + 1) % SLOTS
+    n0 = na + 2
+    slot_a, slot_b = (n0 + ns) % SLOTS, (n0 + ns + 1) % SLOTS
     rest, tail = fs - d, d - wide
     half = wide - tail
     shared_a = [load(ws2.at[:d, :wide], wbuf.at[slot_a], wsem.at[slot_a, 0])]
@@ -103,8 +105,13 @@
         for cp in copies:
             cp.wait()
 
+    own = [load(h_hbm, h_ref, isem.at[0]), load(tab_hbm, tab_ref, isem.at[1]), load(wr_hbm, wr_ref, isem.at[2])]
+    start(own)
     for n in range(SLOTS):
         start(qkv(n, n))
+    pts[0] = jnp.concatenate([idx_ref[j] * cap + slot_ref[j] for j in range(top)]
+                             + [jnp.full((pts.shape[1] - top, t), -1, jnp.int32)], axis=0)
+    ln_a, ln_f, ln_m = (r[...].astype(F32).reshape(1, d) for r in (la_ref, lf_ref, lm_ref))
 
     barrier = pltpu.get_barrier_semaphore()
     for peer in (core, chip):
@@ -113,21 +120,21 @@
 
     rows = t // PIECES
     part = [pl.ds(q * rows, rows) for q in range(PIECES)]
-    far = [send(h_ref.at[part[q]], ub.at[2, part[q]], hs_sem.at[q], hr_sem.at[q], chip) for q in range(PIECES)]
-    near = send(h_ref, ub.at[1], hs_sem.at[PIECES], hr_sem.at[PIECES], core)
+    far = [send(h_hbm.at[part[q]], ub.at[2, part[q]], hs_sem.at[q], hr_sem.at[q], chip) for q in range(PIECES)]
+    near = send(h_hbm, ub.at[1], hs_sem.at[PIECES], hr_sem.at[PIECES], core)
     onward = [send(ub.at[2, part[q]], ub.at[3, part[q]], hs_sem.at[PIECES + 1 + q], hr_sem.at[PIECES + 1 + q], core)
               for q in range(PIECES)]
-    pfar = send(pt_ref, pts.at[2], ps_sem.at[0], pr_sem.at[0], chip)
-    pnear = send(pt_ref, pts.at[1], ps_sem.at[1], pr_sem.at[1], core)
+    pfar = send(pts.at[0], pts.at[2], ps_sem.at[0], pr_sem.at[0], chip)
+    pnear = send(pts.at[0], pts.at[1], ps_sem.at[1], pr_sem.at[1], core)
     ponward = send(pts.at[2], pts.at[3], ps_sem.at[2], pr_sem.at[2], core)
+    start(far)
+    near.start()
+    wait(own)
+
+    xa[...] = _rms(h_ref[...], ln_a)
+    ub[0] = _rms(h_ref[...], ln_m)
     pfar.start()
-    start(far)
     pnear.start()
-    near.start()
-
-    xa[...] = _rms(h_ref[...], ln_ref[0:1, :])
-    ub[0] = _rms(h_ref[...], ln_ref[2:3, :])
-    pts[0] = pt_ref[...]
 
     def heads(i, _):
         slot = lax.rem(i, SLOTS)
@@ -138,7 +145,7 @@
         def _():
             start(qkv(i + SLOTS, slot))
 
-        for k, nxt in enumerate((wo_a, wo_b, unit(0, 0, (na + 2) % SLOTS))):
+        for k, nxt in enumerate((wo_a, wo_b, shared_in(0))):
             @pl.when(i + SLOTS == na + k)
             def _():
                 start(nxt)
@@ -177,16 +184,45 @@
 
     wait(wo_a)
     residual(_dot(sb[:, :d], wbuf[na % SLOTS]), 0)
-    start(unit(0, 1, na % SLOTS))
+    start(shared_in(1))
     wait(wo_b)
     residual(_dot(sb[:, :d], wbuf[(na + 1) % SLOTS, :, :d - wide]), wide)
-    start(unit(1, 0, (na + 1) % SLOTS))
-    xa[...] = _rms(xa[...], ln_ref[1:2, :])
-    pass_on(2)
+    start(shared_in(2))
+    xa[...] = _rms(xa[...], ln_f)
+    off = (n0 + ns + 2) % SLOTS
+
+    for k in range(ns):
+        wait(shared_in(k))
+        w = min(wa, fs - k * wa)
+        z = _dot(xa[...], wbuf[(n0 + k) % SLOTS, :, :2 * w])
+        sb[:, k * wa:k * wa + w] = _silu_mul(z[:, :w], z[:, w:])
+        if k + SLOTS < ns:
+            start(shared_in(k + SLOTS))
+        elif k + SLOTS == ns:
+            start(shared_a)
+        elif k + SLOTS == ns + 1:
+            start(shared_b)
+        else:
+            start(unit(0, 0, off))
+        if k == 0:
+            pass_on(2)
+
+    def add(z, lo):
+        for c in range(z.shape[1] // BLK):
+            base[lo // BLK + c] += z[:, c * BLK:(c + 1) * BLK]
+
+    wait(shared_a)
+    add(_dot(sb[:, :d], wbuf[slot_a]), 0)
+    start(unit(0, 1, slot_a))
+    wait(shared_b)
+    add(_dot(sb[:, :d], wbuf[slot_b, :, :tail]), wide)
+    add(_dot(sb[:, d:], wbuf[slot_b, :rest, tail:]), 0)
+    add(_dot(sb[:, d:], wbuf[slot_b, rest:2 * rest, tail:]), half)
+    start(unit(1, 0, slot_b))
 
     def weigh(k):
         pos = jnp.concatenate([pts[k].astype(F32), jnp.zeros((HEAD - pts.shape[1], t), F32)], axis=0).T
-        lg = _dot(ub[k], wr_ref[...])
+        lg = lax.dot_general(ub[k], wr_ref[...], (((1,), (1,)), ((), ())), preferred_element_type=F32)
         lo = lax.broadcasted_iota(jnp.int32, lg.shape, 1).astype(F32) * cap
         picks = []
         for j in range(top):
@@ -209,7 +245,7 @@
 
     near.wait_recv()
     pnear.wait_recv()
-    ub[1] = _rms(ub[1], ln_ref[2:3, :])
+    ub[1] = _rms(ub[1], ln_m)
 
     def weigh_body(k, _):
         weigh(k)
@@ -219,18 +255,16 @@
     pass_on(3)
     for cp in onward:
         cp.wait_send()
-    ub[2] = _rms(ub[2], ln_ref[2:3, :])
+    ub[2] = _rms(ub[2], ln_m)
     for cp in onward:
         cp.wait_recv()
-    ub[3] = _rms(ub[3], ln_ref[2:3, :])
+    ub[3] = _rms(ub[3], ln_m)
     ponward.wait()
     pfar.wait_send()
     pnear.wait_send()
     near.wait_send()
     for cp in far:
         cp.wait_send()
-
-    off = (na + 2) % SLOTS
 
     def group(g, last):
         for k in range(4):
@@ -278,6 +312,10 @@
 
     def x2x(c):
         return send(sx.at[c], rx.at[c], sx_sem.at[c], rx_sem.at[c], chip)
+
+    def settle(c):
+        d2d(c, 0).wait_recv()
+        base[c] += rd[lax.rem(c, 2), 0]
 
     def chunk(c, _):
         def quad(i, _):
@@ -299,15 +337,14 @@
 
         lax.fori_loop(0, el // GROUP, quad, 0)
 
-        for k in range(SLOTS):
-            @pl.when(c == k + 1)
-            def _():
-                start(shared_in(k))
-
         @pl.when(c >= 2)
         def _():
             for k in range(2):
                 d2d(c - 2, k).wait_send()
+
+        @pl.when(c >= 1)
+        def _():
+            settle(c - 1)
 
         def total(k):
             z = _dot(cm[k], ys[k])
@@ -322,37 +359,13 @@
         d2d(c, 1).wait_recv()
         sx[c] += rd[lax.rem(c, 2), 1]
         x2x(c).start()
-        d2d(c, 0).wait_recv()
-        base[c] += rd[lax.rem(c, 2), 0]
         return 0
 
     lax.fori_loop(0, nc, chunk, 0)
+    settle(nc - 1)
     for c in (nc - 2, nc - 1):
         for k in range(2):
             d2d(c, k).wait_send()
-
-    for k in range(ns):
-        wait(shared_in(k))
-        w = min(wa, fs - k * wa)
-        z = _dot(xa[...], wbuf[k % SLOTS, :, :2 * w])
-        sb[:, k * wa:k * wa + w] = _silu_mul(z[:, :w], z[:, w:])
-        if k + SLOTS < ns:
-            start(shared_in(k + SLOTS))
-        elif k + SLOTS == ns:
-            start(shared_a)
-        elif k + SLOTS == ns + 1:
-            start(shared_b)
-
-    def add(z, lo):
-        for c in range(z.shape[1] // BLK):
-            base[lo // BLK + c] += z[:, c * BLK:(c + 1) * BLK]
-
-    wait(shared_a)
-    add(_dot(sb[:, :d], wbuf[slot_a]), 0)
-    wait(shared_b)
-    add(_dot(sb[:, :d], wbuf[slot_b, :, :tail]), wide)
-    add(_dot(sb[:, d:], wbuf[slot_b, :rest, tail:]), 0)
-    add(_dot(sb[:, d:], wbuf[slot_b, rest:2 * rest, tail:]), half)
 
     def put(c):
         return load(ob.at[c], out_hbm.at[:, pl.ds(pl.multiple_of(c * BLK, BLK), BLK)], osem.at[c])
@@ -386,18 +399,16 @@
         cap = CAP_FACTOR * t * top // (el * mesh.shape['ep'])
         nc = d // BLK
         wide = 2 * ((fe // 2 + HEAD - 1) // HEAD * HEAD)
-        pos = (idx * cap + slot).reshape(t, top)
-        pt = jnp.pad(pos.T, ((0, 8 - top), (0, 0)), constant_values=-1)
-        lns = jnp.stack([ln_attn, ln_ffn, ln_moe]).astype(F32)
         hbm = pl.BlockSpec(memory_space=pl.ANY)
         vmem = pl.BlockSpec(memory_space=pltpu.VMEM)
         dma = pltpu.SemaphoreType.DMA
         out = pl.pallas_call(
             functools.partial(_layer, el, cap, top),
-            in_specs=[vmem] * 5 + [hbm] * 10,
+            in_specs=[vmem] * 5 + [hbm] * 13,
             out_specs=hbm,
             out_shape=jax.ShapeDtypeStruct((t, d), BF16),
             scratch_shapes=[
+                pltpu.VMEM((t, d), BF16), pltpu.VMEM((2, s, HEAD), F32), pltpu.VMEM((wr.shape[1], d), BF16),
                 pltpu.VMEM((SLOTS, d, wide), BF16), pltpu.VMEM((RING, fe, BLK), BF16), pltpu.VMEM((el, 4 * cap, fe), BF16),
                 pltpu.VMEM((4, t, d), BF16), pltpu.VMEM((t, d), BF16), pltpu.VMEM((t, fs), BF16),
                 pltpu.VMEM((GROUP, 4 * cap, d), BF16), pltpu.VMEM((4, el * cap, BLK), BF16),
@@ -405,12 +416,13 @@
                 pltpu.VMEM((2, 2, t, BLK), F32), pltpu.VMEM((2, 2, t, BLK), F32),
                 pltpu.VMEM((nc, t, BLK), F32), pltpu.VMEM((nc, t, BLK), F32), pltpu.VMEM((nc, t, BLK), F32),
                 pltpu.VMEM((nc, t, BLK), BF16),
-                dma((SLOTS, 3)), dma((RING,)), dma((nc,)), dma((2 * PIECES + 1,)), dma((2 * PIECES + 1,)), dma((3,)), dma((3,)),
+                dma((3,)), dma((SLOTS, 3)), dma((RING,)), dma((nc,)), dma((2 * PIECES + 1,)), dma((2 * PIECES + 1,)), dma((3,)), dma((3,)),
                 dma((2, 2)), dma((2, 2)), dma((nc,)), dma((nc,)),
             ],
             compiler_params=pltpu.CompilerParams(collective_id=0, has_side_effects=True, vmem_limit_bytes=67043328),
             name='layer',
-        )(h0.reshape(t, d), pt, lns, jnp.asarray(_tables(s)), wr, wq, wk, wv, wo, ws1, ws3, ws2, ue1, ue3, ue2)
+        )(idx.reshape(t, 1, top).transpose(2, 1, 0), slot.reshape(t, 1, top).transpose(2, 1, 0), ln_attn, ln_ffn, ln_moe,
+          h0.reshape(t, d), jnp.asarray(_tables(s)), wr.T, wq, wk, wv, wo, ws1, ws3, ws2, ue1, ue3, ue2)
         return out.reshape(b, s, d)
 
     specs = (rows, rows, rows) + (rep,) * 11 + (P('ep'), P('ep'), P('ep'))

time: 166 us -> 169 us (1.018)
  Pallas kernels: 157 us -> 166 us
  local copies, waits for them, and re-layouts: 6.93 us -> 2.3 us
    pallas_call x1, Pallas kernels: 157 us -> 166 us  [local(): pl.pallas_call(functools.partial(_layer, el, cap, top), in_specs=[vmem] *...]
    another operation x3 -> x0, local copies, waits for them, and re-layouts: 2.08 us -> none  [local(): lns = jnp.stack([ln_attn, ln_ffn, ln_moe]).astype(F32)]
    unnamed x2 -> x1, local copies, waits for them, and re-layouts: 4.26 us -> 2.3 us
where the time goes in v4:
time: 169 us; the launch traced here: 168 us
  Pallas kernels  166 us (98%)
  local copies, waits for them, and re-layouts  2.3 us (1%)
    pallas_call x1, Pallas kernels, local(): pl.pallas_call(functools.partial(_layer, el, cap, top), in_specs=[vmem] *...  166 us

profile of v4, /device:TPU:0, one launch (start us, length us, event | category | flops | bytes accessed | tf_op | source)
XLA Modules:
  0.0 168.3 jit_solution(5223476444651541238)
XLA Ops:
  0.0 166.0 %layer.1 = bf16[256,2048]{1,0:T(8,128)(2,1)} custom-call(s32[6,1,256]{2,1,0:T(1,128)} %bitcast.12, s32[6,1,256]{2,1,0:T(1,128)} %bitcast.13, bf16[2048]{0:T(1024)(128)(2,1)} %la_ref.1, bf16[2048]{0:T(1024)(128)(2,1)} %lf_ref.1, bf16[2048]{0:T(1024)(128)(2,1)} %lm_ref.1, bf16[256,2048]{1,0:T(8,128)(2,1)} %bitcast.10, f32[2,256,128]{2,1,0:T(8,128)} %constant.2.clone.tab_hbm, ...), custom_call_target="tpu_custom_call" | custom-call | tf_op jit(solution)/shard_map/layer/pallas_call | solution.py:405
  166.0 2.3 %copy.20 = bf16[1,256,2048]{2,1,0:T(8,128)(2,1)} copy(bf16[1,256,2048]{2,1,0:T(8,128)(2,1)} %bitcast.9) | data formatting | bytes 2097152

commit v5 on v4

--- a/solution.py
+++ b/solution.py
@@ -145,7 +145,7 @@
         def _():
             start(qkv(i + SLOTS, slot))
 
-        for k, nxt in enumerate((wo_a, wo_b, shared_in(0))):
+        for k, nxt in enumerate((wo_a, wo_b, unit(0, 0, (na + 2) % SLOTS))):
             @pl.when(i + SLOTS == na + k)
             def _():
                 start(nxt)
@@ -184,41 +184,13 @@
 
     wait(wo_a)
     residual(_dot(sb[:, :d], wbuf[na % SLOTS]), 0)
-    start(shared_in(1))
+    start(unit(0, 1, na % SLOTS))
     wait(wo_b)
     residual(_dot(sb[:, :d], wbuf[(na + 1) % SLOTS, :, :d - wide]), wide)
-    start(shared_in(2))
+    start(unit(1, 0, (na + 1) % SLOTS))
     xa[...] = _rms(xa[...], ln_f)
-    off = (n0 + ns + 2) % SLOTS
-
-    for k in range(ns):
-        wait(shared_in(k))
-        w = min(wa, fs - k * wa)
-        z = _dot(xa[...], wbuf[(n0 + k) % SLOTS, :, :2 * w])
-        sb[:, k * wa:k * wa + w] = _silu_mul(z[:, :w], z[:, w:])
-        if k + SLOTS < ns:
-            start(shared_in(k + SLOTS))
-        elif k + SLOTS == ns:
-            start(shared_a)
-        elif k + SLOTS == ns + 1:
-            start(shared_b)
-        else:
-            start(unit(0, 0, off))
-        if k == 0:
-            pass_on(2)
-
-    def add(z, lo):
-        for c in range(z.shape[1] // BLK):
-            base[lo // BLK + c] += z[:, c * BLK:(c + 1) * BLK]
-
-    wait(shared_a)
-    add(_dot(sb[:, :d], wbuf[slot_a]), 0)
-    start(unit(0, 1, slot_a))
-    wait(shared_b)
-    add(_dot(sb[:, :d], wbuf[slot_b, :, :tail]), wide)
-    add(_dot(sb[:, d:], wbuf[slot_b, :rest, tail:]), 0)
-    add(_dot(sb[:, d:], wbuf[slot_b, rest:2 * rest, tail:]), half)
-    start(unit(1, 0, slot_b))
+    pass_on(2)
+    off = n0 % SLOTS
 
     def weigh(k):
         pos = jnp.concatenate([pts[k].astype(F32), jnp.zeros((HEAD - pts.shape[1], t), F32)], axis=0).T
@@ -337,6 +309,11 @@
 
         lax.fori_loop(0, el // GROUP, quad, 0)
 
+        for k in range(SLOTS):
+            @pl.when(c == k + 1)
+            def _():
+                start(shared_in(k))
+
         @pl.when(c >= 2)
         def _():
             for k in range(2):
@@ -366,6 +343,29 @@
     for c in (nc - 2, nc - 1):
         for k in range(2):
             d2d(c, k).wait_send()
+
+    for k in range(ns):
+        wait(shared_in(k))
+        w = min(wa, fs - k * wa)
+        z = _dot(xa[...], wbuf[(n0 + k) % SLOTS, :, :2 * w])
+        sb[:, k * wa:k * wa + w] = _silu_mul(z[:, :w], z[:, w:])
+        if k + SLOTS < ns:
+            start(shared_in(k + SLOTS))
+        elif k + SLOTS == ns:
+            start(shared_a)
+        elif k + SLOTS == ns + 1:
+            start(shared_b)
+
+    def add(z, lo):
+        for c in range(z.shape[1] // BLK):
+            base[lo // BLK + c] += z[:, c * BLK:(c + 1) * BLK]
+
+    wait(shared_a)
+    add(_dot(sb[:, :d], wbuf[slot_a]), 0)
+    wait(shared_b)
+    add(_dot(sb[:, :d], wbuf[slot_b, :, :tail]), wide)
+    add(_dot(sb[:, d:], wbuf[slot_b, :rest, tail:]), 0)
+    add(_dot(sb[:, d:], wbuf[slot_b, rest:2 * rest, tail:]), half)
 
     def put(c):
         return load(ob.at[c], out_hbm.at[:, pl.ds(pl.multiple_of(c * BLK, BLK), BLK)], osem.at[c])

time: 169 us -> 162 us (0.959)
  Pallas kernels: 166 us -> 159 us
    pallas_call x1, Pallas kernels: 166 us -> 159 us  [local(): pl.pallas_call(functools.partial(_layer, el, cap, top), in_specs=[vmem] *...]
where the time goes in v5:
time: 162 us; the launch traced here: 161 us
  Pallas kernels  159 us (98%)
  local copies, waits for them, and re-layouts  2.3 us (1%)
    pallas_call x1, Pallas kernels, local(): pl.pallas_call(functools.partial(_layer, el, cap, top), in_specs=[vmem] *...  159 us

profile of v5, /device:TPU:0, one launch (start us, length us, event | category | flops | bytes accessed | tf_op | source)
XLA Modules:
  0.0 161.3 jit_solution(16031158508670108928)
XLA Ops:
  0.0 159.0 %layer.1 = bf16[256,2048]{1,0:T(8,128)(2,1)} custom-call(s32[6,1,256]{2,1,0:T(1,128)} %bitcast.12, s32[6,1,256]{2,1,0:T(1,128)} %bitcast.13, bf16[2048]{0:T(1024)(128)(2,1)} %la_ref.1, bf16[2048]{0:T(1024)(128)(2,1)} %lf_ref.1, bf16[2048]{0:T(1024)(128)(2,1)} %lm_ref.1, bf16[256,2048]{1,0:T(8,128)(2,1)} %bitcast.10, f32[2,256,128]{2,1,0:T(8,128)} %constant.2.clone.tab_hbm, ...), custom_call_target="tpu_custom_call" | custom-call | tf_op jit(solution)/shard_map/layer/pallas_call | solution.py:405
  159.0 2.3 %copy.20 = bf16[1,256,2048]{2,1,0:T(8,128)(2,1)} copy(bf16[1,256,2048]{2,1,0:T(8,128)(2,1)} %bitcast.9) | data formatting | bytes 2097152

commit v6 on v5

--- a/solution.py
+++ b/solution.py
@@ -12,10 +12,10 @@
 EPS = 1e-6
 CAP_FACTOR = 2
 BLK = 256
-RING = 8
-SLOTS = 3
+SLOTS = 4
 GROUP = 4
 PIECES = 4
+HOLD = 4
 MESH = pl.DeviceIdType.MESH
 F32, BF16 = jnp.float32, jnp.bfloat16
 
@@ -43,8 +43,8 @@
 
 
 def _layer(el, cap, top, idx_ref, slot_ref, la_ref, lf_ref, lm_ref, h_hbm, tab_hbm, wr_hbm, wq, wk, wv, wo, ws1, ws3, ws2, ue1, ue3, ue2, out_hbm,
-           h_ref, tab_ref, wr_ref, wbuf, ring, he, ub, xa, sb, x4, ys, cm, pts, sd, rd, sx, rx, base, ob,
-           isem, wsem, rsem, osem, hs_sem, hr_sem, ps_sem, pr_sem, sd_sem, rd_sem, sx_sem, rx_sem):
+           h_ref, tab_ref, wr_ref, wbuf, he, ub, xa, sb, x4, ys, cm, pts, sd, rd, sx, rx, base,
+           isem, wsem, osem, hs_sem, hr_sem, ps_sem, pr_sem, sd_sem, rd_sem, sx_sem, rx_sem):
     me = lax.axis_index('ep')
     dp = lax.axis_index('dp')
     core = (dp, me + 1 - 2 * lax.rem(me, 2))
@@ -78,8 +78,10 @@
         return [load(ue.at[e, :, lo:lo + w], wbuf.at[slot, :, k * w:(k + 1) * w], wsem.at[slot, k])
                 for k, ue in enumerate((ue1, ue3))]
 
-    def piece(c, e, slot):
-        return load(ue2.at[e, :, pl.ds(pl.multiple_of(c * BLK, BLK), BLK)], ring.at[slot], rsem.at[slot])
+    def pieces(c, i, slot):
+        cols = pl.ds(pl.multiple_of(c * BLK, BLK), BLK)
+        return [load(ue2.at[GROUP * i + k, :, cols], wbuf.at[slot, :fe, k * BLK:(k + 1) * BLK], wsem.at[slot, k])
+                for k in range(GROUP)]
 
     def shared_in(k):
         lo, w = k * wa, min(wa, fs - k * wa)
@@ -88,7 +90,9 @@
                 for i, ws in enumerate((ws1, ws3))]
 
     ns = -(-fs // wa)
-    n0 = na + 2
+    up0 = na + 2
+    down0 = up0 + 2 * el
+    n0 = down0 + nc * (el // GROUP)
     slot_a, slot_b = (n0 + ns) % SLOTS, (n0 + ns + 1) % SLOTS
     rest, tail = fs - d, d - wide
     half = wide - tail
@@ -141,12 +145,8 @@
         wait(qkv(i, slot))
         z = _dot(xa[...], wbuf[slot])
 
-        @pl.when(i + SLOTS < na)
-        def _():
-            start(qkv(i + SLOTS, slot))
-
-        for k, nxt in enumerate((wo_a, wo_b, unit(0, 0, (na + 2) % SLOTS))):
-            @pl.when(i + SLOTS == na + k)
+        for k, nxt in enumerate((wo_a, wo_b, unit(0, 0, up0 % SLOTS), unit(0, 1, (up0 + 1) % SLOTS))):
+            @pl.when(i == k)
             def _():
                 start(nxt)
 
@@ -184,13 +184,13 @@
 
     wait(wo_a)
     residual(_dot(sb[:, :d], wbuf[na % SLOTS]), 0)
-    start(unit(0, 1, na % SLOTS))
+    start(unit(1, 0, na % SLOTS))
     wait(wo_b)
     residual(_dot(sb[:, :d], wbuf[(na + 1) % SLOTS, :, :d - wide]), wide)
-    start(unit(1, 0, (na + 1) % SLOTS))
+    start(unit(1, 1, (na + 1) % SLOTS))
     xa[...] = _rms(xa[...], ln_f)
     pass_on(2)
-    off = n0 % SLOTS
+    off = up0 % SLOTS
 
     def weigh(k):
         pos = jnp.concatenate([pts[k].astype(F32), jnp.zeros((HEAD - pts.shape[1], t), F32)], axis=0).T
@@ -260,17 +260,14 @@
                 wait(unit(e, h, slot))
                 z = _dot(x4[j], wbuf[slot, :, :2 * w])
                 he[e, :, h * wa:h * wa + w] = _silu_mul(z[:, :w], z[:, w:])
-                en, hn = e + (h + SLOTS) // 2, (h + SLOTS) % 2
-
-                @pl.when(en < el)
+
+                @pl.when(e + 2 < el)
                 def _():
-                    start(unit(en, hn, slot))
-
-                if h == 0:
-                    @pl.when(e == el - 1)
-                    def _():
-                        for n in range(RING):
-                            piece(0, n, n).start()
+                    start(unit(e + 2, h, slot))
+
+                @pl.when(e + 2 >= el)
+                def _():
+                    start(pieces(0, 2 * (e + 2 - el) + h, slot))
             return 0
 
         lax.fori_loop(0, GROUP, ffn_in, 0)
@@ -283,7 +280,8 @@
         return send(sd.at[p, k], rd.at[p, k], sd_sem.at[p, k], rd_sem.at[p, k], core)
 
     def x2x(c):
-        return send(sx.at[c], rx.at[c], sx_sem.at[c], rx_sem.at[c], chip)
+        p = lax.rem(c, HOLD)
+        return send(sx.at[p], rx.at[c], sx_sem.at[p], rx_sem.at[c], chip)
 
     def settle(c):
         d2d(c, 0).wait_recv()
@@ -291,28 +289,25 @@
 
     def chunk(c, _):
         def quad(i, _):
-            s0 = GROUP * lax.rem(i, RING // GROUP)
-            for k in range(GROUP):
-                piece(c, GROUP * i + k, s0 + k).wait()
+            slot = lax.rem(i + down0, SLOTS)
+            wait(pieces(c, i, slot))
             for k in range(GROUP):
                 e = GROUP * i + k
-                y = _dot(he[e], ring[s0 + k]).astype(BF16)
+                y = _dot(he[e], wbuf[slot, :fe, k * BLK:(k + 1) * BLK]).astype(BF16)
                 for b in range(4):
                     ys[b, pl.ds(pl.multiple_of(e * cap, cap), cap), :] = y[b * cap:(b + 1) * cap]
-            wrap = (GROUP * i + RING >= el).astype(jnp.int32)
-
-            @pl.when(c + wrap < nc)
+
+            @pl.when(c + 1 < nc)
             def _():
-                for k in range(GROUP):
-                    piece(c + wrap, lax.rem(GROUP * i + RING, el) + k, s0 + k).start()
+                start(pieces(c + 1, i, slot))
+
+            for k in range(ns):
+                @pl.when(jnp.logical_and(c + 1 == nc, i == k))
+                def _():
+                    start(shared_in(k))
             return 0
 
         lax.fori_loop(0, el // GROUP, quad, 0)
-
-        for k in range(SLOTS):
-            @pl.when(c == k + 1)
-            def _():
-                start(shared_in(k))
 
         @pl.when(c >= 2)
         def _():
@@ -329,12 +324,17 @@
 
         sd[lax.rem(c, 2), 1] = total(3)
         d2d(c, 1).start()
-        sx[c] = total(2)
+
+        @pl.when(c >= HOLD)
+        def _():
+            x2x(c - HOLD).wait_send()
+
+        sx[lax.rem(c, HOLD)] = total(2)
         sd[lax.rem(c, 2), 0] = total(1)
         d2d(c, 0).start()
         base[c] += total(0)
         d2d(c, 1).wait_recv()
-        sx[c] += rd[lax.rem(c, 2), 1]
+        sx[lax.rem(c, HOLD)] += rd[lax.rem(c, 2), 1]
         x2x(c).start()
         return 0
 
@@ -349,11 +349,9 @@
         w = min(wa, fs - k * wa)
         z = _dot(xa[...], wbuf[(n0 + k) % SLOTS, :, :2 * w])
         sb[:, k * wa:k * wa + w] = _silu_mul(z[:, :w], z[:, w:])
-        if k + SLOTS < ns:
-            start(shared_in(k + SLOTS))
-        elif k + SLOTS == ns:
+        if k == 0:
             start(shared_a)
-        elif k + SLOTS == ns + 1:
+        elif k == 1:
             start(shared_b)
 
     def add(z, lo):
@@ -368,18 +366,20 @@
     add(_dot(sb[:, d:], wbuf[slot_b, rest:2 * rest, tail:]), half)
 
     def put(c):
-        return load(ob.at[c], out_hbm.at[:, pl.ds(pl.multiple_of(c * BLK, BLK), BLK)], osem.at[c])
+        cols = pl.ds(pl.multiple_of(c * BLK, BLK), BLK)
+        return load(xa.at[:, cols], out_hbm.at[:, cols], osem.at[c])
 
     def finish(c, _):
         x2x(c).wait_recv()
-        ob[c] = (base[c] + rx[c]).astype(BF16)
+        xa[:, pl.ds(pl.multiple_of(c * BLK, BLK), BLK)] = (base[c] + rx[c]).astype(BF16)
         put(c).start()
         return 0
 
     lax.fori_loop(0, nc, finish, 0)
+    for c in range(nc - HOLD, nc):
+        x2x(c).wait_send()
 
     def drain(c, _):
-        x2x(c).wait_send()
         put(c).wait()
         return 0
 
@@ -409,15 +409,14 @@
             out_shape=jax.ShapeDtypeStruct((t, d), BF16),
             scratch_shapes=[
                 pltpu.VMEM((t, d), BF16), pltpu.VMEM((2, s, HEAD), F32), pltpu.VMEM((wr.shape[1], d), BF16),
-                pltpu.VMEM((SLOTS, d, wide), BF16), pltpu.VMEM((RING, fe, BLK), BF16), pltpu.VMEM((el, 4 * cap, fe), BF16),
+                pltpu.VMEM((SLOTS, d, wide), BF16), pltpu.VMEM((el, 4 * cap, fe), BF16),
                 pltpu.VMEM((4, t, d), BF16), pltpu.VMEM((t, d), BF16), pltpu.VMEM((t, fs), BF16),
                 pltpu.VMEM((GROUP, 4 * cap, d), BF16), pltpu.VMEM((4, el * cap, BLK), BF16),
                 pltpu.VMEM((4, 3 * t, el * cap), BF16), pltpu.VMEM((4, 8, t), jnp.int32),
                 pltpu.VMEM((2, 2, t, BLK), F32), pltpu.VMEM((2, 2, t, BLK), F32),
-                pltpu.VMEM((nc, t, BLK), F32), pltpu.VMEM((nc, t, BLK), F32), pltpu.VMEM((nc, t, BLK), F32),
-                pltpu.VMEM((nc, t, BLK), BF16),
-                dma((3,)), dma((SLOTS, 3)), dma((RING,)), dma((nc,)), dma((2 * PIECES + 1,)), dma((2 * PIECES + 1,)), dma((3,)), dma((3,)),
-                dma((2, 2)), dma((2, 2)), dma((nc,)), dma((nc,)),
+                pltpu.VMEM((HOLD, t, BLK), F32), pltpu.VMEM((nc, t, BLK), F32), pltpu.VMEM((nc, t, BLK), F32),
+                dma((3,)), dma((SLOTS, GROUP)), dma((nc,)), dma((2 * PIECES + 1,)), dma((2 * PIECES + 1,)), dma((3,)), dma((3,)),
+                dma((2, 2)), dma((2, 2)), dma((HOLD,)), dma((nc,)),
             ],
             compiler_params=pltpu.CompilerParams(collective_id=0, has_side_effects=True, vmem_limit_bytes=67043328),
             name='layer',

time: 162 us -> 152 us (0.938)
  Pallas kernels: 159 us -> 150 us
    pallas_call x1, Pallas kernels: 159 us -> 150 us  [local(): pl.pallas_call(functools.partial(_layer, el, cap, top), in_specs=[vmem] *...]
where the time goes in v6:
time: 152 us
  Pallas kernels  150 us (99%)
  local copies, waits for them, and re-layouts  2.3 us (2%)
    pallas_call x1, Pallas kernels, local(): pl.pallas_call(functools.partial(_layer, el, cap, top), in_specs=[vmem] *...  150 us

profile of v6, /device:TPU:0, one launch (start us, length us, event | category | flops | bytes accessed | tf_op | source)
XLA Modules:
  0.0 151.9 jit_solution(1203514934544985707)
XLA Ops:
  0.0 149.6 %layer.1 = bf16[256,2048]{1,0:T(8,128)(2,1)} custom-call(s32[6,1,256]{2,1,0:T(1,128)} %bitcast.12, s32[6,1,256]{2,1,0:T(1,128)} %bitcast.13, bf16[2048]{0:T(1024)(128)(2,1)} %la_ref.1, bf16[2048]{0:T(1024)(128)(2,1)} %lf_ref.1, bf16[2048]{0:T(1024)(128)(2,1)} %lm_ref.1, bf16[256,2048]{1,0:T(8,128)(2,1)} %bitcast.10, f32[2,256,128]{2,1,0:T(8,128)} %constant.2.clone.tab_hbm, ...), custom_call_target="tpu_custom_call" | custom-call | tf_op jit(solution)/shard_map/layer/pallas_call | solution.py:405
  149.6 2.3 %copy.20 = bf16[1,256,2048]{2,1,0:T(8,128)(2,1)} copy(bf16[1,256,2048]{2,1,0:T(8,128)(2,1)} %bitcast.9) | data formatting | bytes 2097152

commit v7 on v6

--- a/solution.py
+++ b/solution.py
@@ -219,11 +219,6 @@
     pnear.wait_recv()
     ub[1] = _rms(ub[1], ln_m)
 
-    def weigh_body(k, _):
-        weigh(k)
-        return 0
-
-    lax.fori_loop(0, 2, weigh_body, 0)
     pass_on(3)
     for cp in onward:
         cp.wait_send()
@@ -239,6 +234,7 @@
         cp.wait_send()
 
     def group(g, last):
+        weigh(g)
         for k in range(4):
             r = lax.broadcasted_iota(jnp.int32, (GROUP * cap, t), 0) + (first + g * (GROUP * cap))
             hit = pts[k, 0:1, :] == r
@@ -248,10 +244,6 @@
             for j in range(GROUP):
                 x4[j, k * cap:(k + 1) * cap, :] = x[j * cap:(j + 1) * cap]
 
-        @pl.when(g < 2)
-        def _():
-            weigh(g + 2)
-
         def ffn_in(j, _):
             e = g * GROUP + j
             for h in range(2):
@@ -288,26 +280,30 @@
         base[c] += rd[lax.rem(c, 2), 0]
 
     def chunk(c, _):
-        def quad(i, _):
-            slot = lax.rem(i + down0, SLOTS)
-            wait(pieces(c, i, slot))
-            for k in range(GROUP):
-                e = GROUP * i + k
-                y = _dot(he[e], wbuf[slot, :fe, k * BLK:(k + 1) * BLK]).astype(BF16)
-                for b in range(4):
-                    ys[b, pl.ds(pl.multiple_of(e * cap, cap), cap), :] = y[b * cap:(b + 1) * cap]
+        def duo(m, _):
+            steps = [(2 * m + q, lax.rem(2 * m + q + down0, SLOTS)) for q in range(2)]
+            for i, slot in steps:
+                wait(pieces(c, i, slot))
+            for i, slot in steps:
+                for k in range(GROUP):
+                    e = GROUP * i + k
+                    y = _dot(he[e], wbuf[slot, :fe, k * BLK:(k + 1) * BLK]).astype(BF16)
+                    for b in range(4):
+                        ys[b, pl.ds(pl.multiple_of(e * cap, cap), cap), :] = y[b * cap:(b + 1) * cap]
 
             @pl.when(c + 1 < nc)
             def _():
-                start(pieces(c + 1, i, slot))
-
-            for k in range(ns):
-                @pl.when(jnp.logical_and(c + 1 == nc, i == k))
+                for i, slot in steps:
+                    start(pieces(c + 1, i, slot))
+
+            for k in range(ns // 2):
+                @pl.when(jnp.logical_and(c + 1 == nc, m == k))
                 def _():
-                    start(shared_in(k))
+                    start(shared_in(2 * k))
+                    start(shared_in(2 * k + 1))
             return 0
 
-        lax.fori_loop(0, el // GROUP, quad, 0)
+        lax.fori_loop(0, el // GROUP // 2, duo, 0)
 
         @pl.when(c >= 2)
         def _():

time: 152 us -> 146 us (0.961)
  Pallas kernels: 150 us -> 144 us
    pallas_call x1, Pallas kernels: 150 us -> 144 us  [local(): pl.pallas_call(functools.partial(_layer, el, cap, top), in_specs=[vmem] *...]
where the time goes in v7:
time: 146 us
  Pallas kernels  144 us (99%)
  local copies, waits for them, and re-layouts  2.3 us (2%)
    pallas_call x1, Pallas kernels, local(): pl.pallas_call(functools.partial(_layer, el, cap, top), in_specs=[vmem] *...  144 us

profile of v7, /device:TPU:0, one launch (start us, length us, event | category | flops | bytes accessed | tf_op | source)
XLA Modules:
  0.0 146.3 jit_solution(3709383223669094848)
XLA Ops:
  0.0 143.9 %layer.1 = bf16[256,2048]{1,0:T(8,128)(2,1)} custom-call(s32[6,1,256]{2,1,0:T(1,128)} %bitcast.12, s32[6,1,256]{2,1,0:T(1,128)} %bitcast.13, bf16[2048]{0:T(1024)(128)(2,1)} %la_ref.1, bf16[2048]{0:T(1024)(128)(2,1)} %lf_ref.1, bf16[2048]{0:T(1024)(128)(2,1)} %lm_ref.1, bf16[256,2048]{1,0:T(8,128)(2,1)} %bitcast.10, f32[2,256,128]{2,1,0:T(8,128)} %constant.2.clone.tab_hbm, ...), custom_call_target="tpu_custom_call" | custom-call | tf_op jit(solution)/shard_map/layer/pallas_call | solution.py:401
  144.0 2.3 %copy.20 = bf16[1,256,2048]{2,1,0:T(8,128)(2,1)} copy(bf16[1,256,2048]{2,1,0:T(8,128)(2,1)} %bitcast.9) | data formatting | bytes 2097152

commit v8 on v7

--- a/solution.py
+++ b/solution.py
@@ -16,6 +16,7 @@
 GROUP = 4
 PIECES = 4
 HOLD = 4
+EARLY = 2
 MESH = pl.DeviceIdType.MESH
 F32, BF16 = jnp.float32, jnp.bfloat16
 
@@ -85,15 +86,15 @@
 
     def shared_in(k):
         lo, w = k * wa, min(wa, fs - k * wa)
-        n = (n0 + k) % SLOTS
+        n = (na + 2 + k) % SLOTS
         return [load(ws.at[:, lo:lo + w], wbuf.at[n, :, i * w:(i + 1) * w], wsem.at[n, i])
                 for i, ws in enumerate((ws1, ws3))]
 
     ns = -(-fs // wa)
-    up0 = na + 2
+    up0 = na + 2 + EARLY
     down0 = up0 + 2 * el
     n0 = down0 + nc * (el // GROUP)
-    slot_a, slot_b = (n0 + ns) % SLOTS, (n0 + ns + 1) % SLOTS
+    slot_a, slot_b = (n0 + ns - EARLY) % SLOTS, (n0 + ns - EARLY + 1) % SLOTS
     rest, tail = fs - d, d - wide
     half = wide - tail
     shared_a = [load(ws2.at[:d, :wide], wbuf.at[slot_a], wsem.at[slot_a, 0])]
@@ -145,7 +146,7 @@
         wait(qkv(i, slot))
         z = _dot(xa[...], wbuf[slot])
 
-        for k, nxt in enumerate((wo_a, wo_b, unit(0, 0, up0 % SLOTS), unit(0, 1, (up0 + 1) % SLOTS))):
+        for k, nxt in enumerate((wo_a, wo_b, shared_in(0), shared_in(1))):
             @pl.when(i == k)
             def _():
                 start(nxt)
@@ -184,12 +185,23 @@
 
     wait(wo_a)
     residual(_dot(sb[:, :d], wbuf[na % SLOTS]), 0)
-    start(unit(1, 0, na % SLOTS))
+    start(unit(0, 0, up0 % SLOTS))
     wait(wo_b)
     residual(_dot(sb[:, :d], wbuf[(na + 1) % SLOTS, :, :d - wide]), wide)
-    start(unit(1, 1, (na + 1) % SLOTS))
+    start(unit(0, 1, (up0 + 1) % SLOTS))
     xa[...] = _rms(xa[...], ln_f)
+
+    def shared_up(k):
+        wait(shared_in(k))
+        w = min(wa, fs - k * wa)
+        z = _dot(xa[...], wbuf[(na + 2 + k) % SLOTS, :, :2 * w])
+        sb[:, k * wa:k * wa + w] = _silu_mul(z[:, :w], z[:, w:])
+
+    shared_up(0)
+    start(unit(1, 0, (up0 + 2) % SLOTS))
     pass_on(2)
+    shared_up(1)
+    start(unit(1, 1, (up0 + 3) % SLOTS))
     off = up0 % SLOTS
 
     def weigh(k):
@@ -296,11 +308,10 @@
                 for i, slot in steps:
                     start(pieces(c + 1, i, slot))
 
-            for k in range(ns // 2):
+            for k, late in enumerate((shared_in(2) + shared_in(3), shared_a + shared_b)):
                 @pl.when(jnp.logical_and(c + 1 == nc, m == k))
                 def _():
-                    start(shared_in(2 * k))
-                    start(shared_in(2 * k + 1))
+                    start(late)
             return 0
 
         lax.fori_loop(0, el // GROUP // 2, duo, 0)
@@ -340,15 +351,8 @@
         for k in range(2):
             d2d(c, k).wait_send()
 
-    for k in range(ns):
-        wait(shared_in(k))
-        w = min(wa, fs - k * wa)
-        z = _dot(xa[...], wbuf[(n0 + k) % SLOTS, :, :2 * w])
-        sb[:, k * wa:k * wa + w] = _silu_mul(z[:, :w], z[:, w:])
-        if k == 0:
-            start(shared_a)
-        elif k == 1:
-            start(shared_b)
+    for k in range(EARLY, ns):
+        shared_up(k)
 
     def add(z, lo):
         for c in range(z.shape[1] // BLK):
@@ -363,11 +367,11 @@
 
     def put(c):
         cols = pl.ds(pl.multiple_of(c * BLK, BLK), BLK)
-        return load(xa.at[:, cols], out_hbm.at[:, cols], osem.at[c])
+        return load(base.at[c], out_hbm.at[:, cols], osem.at[c])
 
     def finish(c, _):
         x2x(c).wait_recv()
-        xa[:, pl.ds(pl.multiple_of(c * BLK, BLK), BLK)] = (base[c] + rx[c]).astype(BF16)
+        base[c] += rx[c]
         put(c).start()
         return 0
 
@@ -402,7 +406,7 @@
             functools.partial(_layer, el, cap, top),
             in_specs=[vmem] * 5 + [hbm] * 13,
             out_specs=hbm,
-            out_shape=jax.ShapeDtypeStruct((t, d), BF16),
+            out_shape=jax.ShapeDtypeStruct((t, d), F32),
             scratch_shapes=[
                 pltpu.VMEM((t, d), BF16), pltpu.VMEM((2, s, HEAD), F32), pltpu.VMEM((wr.shape[1], d), BF16),
                 pltpu.VMEM((SLOTS, d, wide), BF16), pltpu.VMEM((el, 4 * cap, fe), BF16),
@@ -418,7 +422,7 @@
             name='layer',
         )(idx.reshape(t, 1, top).transpose(2, 1, 0), slot.reshape(t, 1, top).transpose(2, 1, 0), ln_attn, ln_ffn, ln_moe,
           h0.reshape(t, d), jnp.asarray(_tables(s)), wr.T, wq, wk, wv, wo, ws1, ws3, ws2, ue1, ue3, ue2)
-        return out.reshape(b, s, d)
+        return out.astype(BF16).reshape(b, s, d)
 
     specs = (rows, rows, rows) + (rep,) * 11 + (P('ep'), P('ep'), P('ep'))
     return jax.shard_map(local, mesh=mesh, in_specs=specs, out_specs=rows, check_vma=False)

time: 146 us -> 151 us (1.034)
  Pallas kernels: 144 us -> 148 us
  other arithmetic: 0 us -> 2.71 us
  local copies, waits for them, and re-layouts: 2.3 us -> 0 us
    pallas_call x1, Pallas kernels: 144 us -> 148 us  [local(): pl.pallas_call(functools.partial(_layer, el, cap, top), in_specs=[vmem] *...]
    reshape x0 -> x1, other arithmetic: none -> 2.71 us  [local(): return out.astype(BF16).reshape(b, s, d)]
    unnamed x1 -> x0, local copies, waits for them, and re-layouts: 2.3 us -> none
where the time goes in v8:
time: 151 us; the launch traced here: 150 us
  Pallas kernels  148 us (98%)
  other arithmetic  2.71 us (2%)
    pallas_call x1, Pallas kernels, local(): pl.pallas_call(functools.partial(_layer, el, cap, top), in_specs=[vmem] *...  148 us

profile of v8, /device:TPU:0, one launch (start us, length us, event | category | flops | bytes accessed | tf_op | source)
XLA Modules:
  0.0 150.4 jit_solution(15348138036239989101)
XLA Ops:
  0.0 147.6 %layer.1 = f32[256,2048]{1,0:T(8,128)} custom-call(s32[6,1,256]{2,1,0:T(1,128)} %bitcast.12, s32[6,1,256]{2,1,0:T(1,128)} %bitcast.13, bf16[2048]{0:T(1024)(128)(2,1)} %la_ref.1, bf16[2048]{0:T(1024)(128)(2,1)} %lf_ref.1, bf16[2048]{0:T(1024)(128)(2,1)} %lm_ref.1, bf16[256,2048]{1,0:T(8,128)(2,1)} %bitcast.10, f32[2,256,128]{2,1,0:T(8,128)} %constant.2.clone.tab_hbm, ...), custom_call_target="tpu_custom_call" | custom-call | tf_op jit(solution)/shard_map/layer/pallas_call | solution.py:405
  147.6 2.7 %convert_bitcast_fusion = bf16[1,256,2048]{2,1,0:T(8,128)(2,1)} fusion(f32[256,2048]{1,0:T(8,128)} %layer.1), kind=kLoop, calls=%fused_computation | loop fusion | flops 524288 | bytes 3145728 | tf_op jit(solution)/shard_map/reshape | solution.py:425
